TPU v7x, 8 devices: a whole 2x2x1 slice. The times are simulated.
8 devices in a mesh: dp: 2 (over z, y), tp: 4 (over x, core).
Axes of the slice: x: 2, y: 2, z: 1, core: 2. Of those that a mesh axis runs over, the one named last changes fastest.
Arguments:
- hidden: bfloat16 [2, 256, 2048], P('dp'), parts along dimension 0
- norm_w: bfloat16 [2, 2048], replicated
- w_z: bfloat16 [2, 2048, 4096], P(None, None, 'tp')
- w_x: bfloat16 [2, 2048, 4096], P(None, None, 'tp')
- w_bc: bfloat16 [2, 2048, 128], replicated
- w_dt: bfloat16 [2, 2048, 64], P(None, None, 'tp')
- conv_x: bfloat16 [2, 4, 4096], P(None, None, 'tp')
- conv_bc: bfloat16 [2, 4, 128], replicated
- bias_x: bfloat16 [2, 4096], P(None, 'tp')
- bias_bc: bfloat16 [2, 128], replicated
- dt_bias: float32 [2, 64], P(None, 'tp')
- a_log: float32 [2, 64], P(None, 'tp')
- d_skip: float32 [2, 64], P(None, 'tp')
- gate_w: bfloat16 [2, 4096], P(None, 'tp')
- w_out: bfloat16 [2, 4096, 2048], P(None, 'tp')
Outputs:
- output: bfloat16 [2, 256, 2048], P('dp'), parts along dimension 0
There are 2 independent parts. A program takes and returns all parts, laid end to end along the dimension named above; an argument that names none is the same for every part.
All inputs are finite; a program needn't handle non-finite values.
Results may differ from a plain program's by a relative error of at most 0.0143168.
Values sent between devices are 32-bit elements.
A program may use at most 1 GiB of HBM per device.

v0:
```python
import jax
import jax.numpy as jnp
from jax import lax
from jax.sharding import PartitionSpec as P

EPSILON = 1e-5
CONV_WIDTH = 4
BLOCK_LEN = 256
FULL_PRECISION = lax.Precision.HIGHEST


def causal_conv(seq_in, kernel, conv_bias):
    n_steps = seq_in.shape[1]
    padded = jnp.pad(seq_in, ((0, 0), (CONV_WIDTH - 1, 0), (0, 0)))
    conv_sum = conv_bias.astype(jnp.float32)
    for tap_index in range(CONV_WIDTH):
        conv_sum = conv_sum + padded[:, tap_index:tap_index + n_steps, :].astype(jnp.float32) * kernel[tap_index].astype(jnp.float32)
    return conv_sum


def ssd_blocks(x_heads, dt_val, a_vals, b_in, c_in):
    n_batch, n_steps, n_heads, head_width = x_heads.shape
    n_state = b_in.shape[-1]
    n_blocks = n_steps // BLOCK_LEN
    x_blocks = x_heads.reshape(n_batch, n_blocks, BLOCK_LEN, n_heads, head_width)
    dt_blocks = dt_val.reshape(n_batch, n_blocks, BLOCK_LEN, n_heads)
    b_blocks = b_in.reshape(n_batch, n_blocks, BLOCK_LEN, n_state)
    c_blocks = c_in.reshape(n_batch, n_blocks, BLOCK_LEN, n_state)
    a_cum = jnp.cumsum(a_vals.reshape(n_batch, n_blocks, BLOCK_LEN, n_heads), axis=2)
    a_cum_t = jnp.swapaxes(a_cum, 2, 3)
    seg_sum = a_cum_t[..., :, None] - a_cum_t[..., None, :]
    step_ids = jnp.arange(BLOCK_LEN)
    lower_tri = step_ids[:, None] >= step_ids[None, :]
    c_dot_b = jnp.einsum('bcin,bcjn->bcij', c_blocks, b_blocks, precision=FULL_PRECISION)
    mix_mat = jnp.where(lower_tri, jnp.exp(jnp.minimum(seg_sum, 0.0)), 0.0) * c_dot_b[:, :, None]
    x_dt = x_blocks * dt_blocks[..., None]
    y_in = jnp.einsum('bchij,bcjhp->bcihp', mix_mat, x_dt, precision=FULL_PRECISION)
    a_last = a_cum[:, :, -1, :]
    tail_decay = jnp.exp(a_last[:, :, None, :] - a_cum)
    block_states = jnp.einsum('bcjn,bcjhp->bchpn', b_blocks, x_dt * tail_decay[..., None], precision=FULL_PRECISION)
    block_ends = jnp.swapaxes(jnp.cumsum(a_last, axis=1), 1, 2)
    block_starts = block_ends - jnp.swapaxes(a_last, 1, 2)
    block_ids = jnp.arange(n_blocks)
    earlier = block_ids[:, None] > block_ids[None, :]
    carry_mat = jnp.where(earlier, jnp.exp(jnp.minimum(block_starts[..., :, None] - block_ends[..., None, :], 0.0)), 0.0)
    s_in = jnp.einsum('bhck,bkhpn->bchpn', carry_mat, block_states, precision=FULL_PRECISION)
    y_st = jnp.einsum('bcin,bchpn->bcihp', c_blocks, s_in, precision=FULL_PRECISION) * jnp.exp(a_cum)[..., None]
    return (y_in + y_st).reshape(n_batch, n_steps, n_heads, head_width)


def mixer_layer(current, norm_w, w_z, w_x, w_bc, w_dt, conv_x, conv_bc, bias_x, bias_bc, dt_bias, a_log, d_skip, gate_w, w_out, inner_width):
    n_batch = current.shape[0]
    n_steps = current.shape[1]
    n_heads = dt_bias.shape[0]
    local_width = w_x.shape[-1]
    state_dim = w_bc.shape[-1] // 2
    residual = current.astype(jnp.float32)
    normed = (residual * lax.rsqrt(jnp.mean(residual * residual, axis=-1, keepdims=True) + EPSILON) * norm_w.astype(jnp.float32)).astype(jnp.bfloat16)
    gate_z = jnp.einsum('btd,de->bte', normed, w_z, preferred_element_type=jnp.float32).astype(jnp.bfloat16)
    x_pre = jnp.einsum('btd,de->bte', normed, w_x, preferred_element_type=jnp.float32).astype(jnp.bfloat16)
    bc_pre = jnp.einsum('btd,de->bte', normed, w_bc, preferred_element_type=jnp.float32).astype(jnp.bfloat16)
    dt_pre = jnp.einsum('btd,de->bte', normed, w_dt, preferred_element_type=jnp.float32).astype(jnp.bfloat16)
    x_act = jax.nn.silu(causal_conv(x_pre, conv_x, bias_x))
    bc_act = jax.nn.silu(causal_conv(bc_pre, conv_bc, bias_bc))
    dt_val = jax.nn.softplus(dt_pre.astype(jnp.float32) + dt_bias)
    a_vals = -dt_val * jnp.exp(a_log)
    x_heads = x_act.reshape(n_batch, n_steps, n_heads, local_width // n_heads)
    y_heads = ssd_blocks(x_heads, dt_val, a_vals, bc_act[..., :state_dim], bc_act[..., state_dim:]) + d_skip[:, None] * x_heads
    gated_v = y_heads.reshape(n_batch, n_steps, local_width) * jax.nn.silu(gate_z.astype(jnp.float32))
    part_sq = jnp.sum(gated_v * gated_v, axis=-1, keepdims=True)
    total_sq = lax.psum(part_sq, 'tp')
    normed_y = (gated_v * lax.rsqrt(total_sq / inner_width + EPSILON) * gate_w.astype(jnp.float32)).astype(jnp.bfloat16)
    part_out = jnp.einsum('bte,ed->btd', normed_y, w_out, preferred_element_type=jnp.float32)
    full_out = lax.psum(part_out, 'tp')
    return (residual + full_out).astype(jnp.bfloat16)


def solution(mesh):
    tp_size = mesh.shape['tp']
    rep_spec = P()
    col_spec = P(None, None, 'tp')
    vec_spec = P(None, 'tp')
    in_specs = (P('dp'), rep_spec, col_spec, col_spec, rep_spec, col_spec, col_spec, rep_spec, vec_spec, rep_spec, vec_spec, vec_spec, vec_spec, vec_spec, P(None, 'tp', None))

    def device_forward(hidden, norm_w, w_z, w_x, w_bc, w_dt, conv_x, conv_bc, bias_x, bias_bc, dt_bias, a_log, d_skip, gate_w, w_out):
        inner_width = w_x.shape[-1] * tp_size
        current = hidden
        for layer_idx in range(norm_w.shape[0]):
            current = mixer_layer(current, norm_w[layer_idx], w_z[layer_idx], w_x[layer_idx], w_bc[layer_idx], w_dt[layer_idx], conv_x[layer_idx], conv_bc[layer_idx], bias_x[layer_idx], bias_bc[layer_idx], dt_bias[layer_idx], a_log[layer_idx], d_skip[layer_idx], gate_w[layer_idx], w_out[layer_idx], inner_width)
        return current

    return jax.shard_map(device_forward, mesh=mesh, in_specs=in_specs, out_specs=P('dp'), check_vma=False)
```

profile of v0, /device:TPU:0, one launch (start us, length us, event | category | flops | bytes accessed | tf_op | source)
XLA Modules:
  0.0 214.0 jit_solution(12653310407112711577)
XLA Ops:
  6.5 1.4 slice_convert_fusion
  7.9 1.5 fusion.36
  9.5 1.3 slice_bitcast_fusion.5
  10.7 1.3 exponential_bitcast_fusion
  12.1 1.7 compare_select_fusion.1
  13.8 0.6 reduce-window.14
  14.4 0.2 slice_reduce_fusion.1
  14.6 0.6 copy.48
  15.2 0.6 iota_compare_fusion
  15.9 0.1 copy.49
  16.1 0.6 fusion.150
  16.7 0.3 slice_reduce_fusion.3
  17.0 0.1 subtract_exponential_fusion.1
  17.2 1.3 copy.52
  18.6 1.3 copy.50
  19.9 3.6 %fusion.68 = bf16[256,1024]{1,0:T(8,128)(2,1)S(1)} fusion(bf16[2,2048,1024]{2,1,0:T(8,128)(2,1)} %param.18, bf16[1,256,2048]{2,1,0:T(8,128)(2,1)S(1)} %copy-done, f32[2048]{0:T(1024)S(1)} %bitcast.321, f32[256]{0:T(256)S(1)} %add_rsqrt_fusion.3), kind=kOutput, calls=%fused_computation.68 | convolution fusion | flops 1076101120 | bytes 5776384 | tf_op jit(solution)/shard_map/btd,de->bte/dot_general | solution.py:60
  23.6 0.6 slice_convert_fusion.6
  24.2 0.6 slice_convert_fusion.7
  24.8 1.8 multiply_multiply_fusion.1
  26.6 1.6 copy.53
  28.2 1.6 convolution_convert_fusion.1
  29.9 0.6 bitcast_convert_fusion.3
  30.4 0.6 bitcast_convert_fusion.4
  31.0 0.2 divide_multiply_fusion.3
  31.2 0.4 fusion.120
  31.7 1.8 convolution_multiply_fusion.3
  33.5 1.3 copy.46
  34.8 1.0 fusion.61
  35.8 7.0 %fusion.65 = f32[1,1,256,16,64]{2,4,3,1,0:T(8,128)} fusion(f32[1,1,256,16,64]{2,4,3,1,0:T(8,128)S(1)} %fusion.61, f32[256,256]{1,0:T(8,128)S(1)} %fusion.120, f32[16,256]{1,0:T(8,128)S(1)} %bitcast_add_fusion.5, pred[256,256]{1,0:T(8,128)(4,1)S(1)} %copy-done.10, f32[256,16,64]{0,2,1:T(8,128)} %bitcast.289, f32[256,16]{0,1:T(8,128)S(1)} %copy-done.6), kind=kOutput, calls=%fused_computation.63 | convolution fusion | flops 810024960 | bytes 3506176 | tf_op jit(solution)/shard_map/bchij,bcjhp->bcihp/dot_general | solution.py:37
  42.8 1.6 copy.54
  44.6 4.7 %multiply_reduce_fusion.1 = (f32[256]{0:T(256)S(1)}, f32[256,1024]{1,0:T(8,128)}) fusion(bf16[2,2048,1024]{2,1,0:T(8,128)(2,1)} %param.17, bf16[1,256,2048]{2,1,0:T(8,128)(2,1)S(1)} %copy-done, f32[2048]{0:T(1024)S(1)} %bitcast.323, f32[256]{0:T(256)S(1)} %copy-done.38, f32[256,1024]{1,0:T(8,128)S(1)} %copy.54, f32[1,256,1024]{2,1,0:T(8,128)S(1)} %get-tuple-element.14, ...), kind=kOutput, calls=%fused_computation.104 | convolution fusion | flops 1078722304 | bytes 8402944 | tf_op jit(solution)/shard_map/btd,de->bte/dot_general | solution.py:59
  49.3 8.7 %psum.28 = f32[1,256,1]{1,2,0:T(1,128)S(1)} all-reduce(f32[1,256,1]{1,2,0:T(1,128)S(1)} %bitcast.328), channel_id=1, replica_groups=mesh['dp'=2,'tp'=4] {'tp'}, use_global_device_ids=true, to_apply=%region_4.5 | all-reduce | flops 256 | bytes 2048 | tf_op jit(solution)/shard_map/psum | solution.py:71
  58.0 0.6 slice_convert_fusion.2
  58.6 5.2 %fusion.30 = f32[1,256,2048]{2,1,0:T(8,128)} fusion(bf16[2,1024,2048]{2,1,0:T(8,128)(2,1)} %param.29, f32[256,1024]{1,0:T(8,128)} %get-tuple-element.46, f32[1024]{0:T(1024)S(1)} %bitcast.327, f32[256]{0:T(256)S(1)} %bitcast.330), kind=kOutput, calls=%fused_computation.36 | convolution fusion | flops 1074528256 | bytes 7345152 | tf_op jit(solution)/shard_map/bte,ed->btd/dot_general | solution.py:73
  63.9 0.7 mul.623
  64.6 45.1 %all-reduce.7.cloned.1.call-done = f32[1,256,2048]{2,1,0:T(8,128)} async-done(((f32[1,256,2048]{2,1,0:T(8,128)}), f32[1,256,2048]{2,1,0:T(8,128)}) %all-reduce.7.cloned.1.call-update) | async-done | bytes 2097168 | tf_op jit(solution)/shard_map/psum | solution.py:74
  109.7 2.0 fusion.40
  111.7 0.5 compare_select_fusion
  112.3 0.7 reduce-window.16
  113.0 0.2 slice_reduce_fusion
  113.1 0.6 copy.57
  113.7 1.6 convolution_convert_fusion
  115.4 4.3 %fusion.74 = bf16[256,1024]{1,0:T(8,128)(2,1)} fusion(bf16[2,2048,1024]{2,1,0:T(8,128)(2,1)} %param.18, bf16[1,256,2048]{2,1,0:T(8,128)(2,1)S(1)} %get-tuple-element.10, f32[2048]{0:T(1024)S(1)} %bitcast.318, f32[256]{0:T(256)S(1)} %add_rsqrt_fusion.1), kind=kOutput, calls=%fused_computation.70 | convolution fusion | flops 1076101120 | bytes 5776384 | tf_op jit(solution)/shard_map/btd,de->bte/dot_general | solution.py:60
  119.7 0.1 copy.58
  119.9 0.6 fusion.148
  120.5 0.3 slice_reduce_fusion.2
  120.8 0.1 subtract_exponential_fusion
  121.0 0.3 copy.61
  121.5 1.3 copy.59
  122.8 3.8 %multiply_multiply_fusion = (f32[1,256,1024]{2,1,0:T(8,128)}, f32[1,256,1024]{2,1,0:T(8,128)S(1)}) fusion(f32[1,256,1024]{2,1,0:T(8,128)S(1)} %copy.61, f32[1,256,1024]{2,1,0:T(8,128)} %copy.59, f32[1024]{0:T(1024)S(1)} %bitcast.308, bf16[256,1024]{1,0:T(8,128)(2,1)} %fusion.74, f32[1024]{0:T(1024)S(1)} %bitcast.309, f32[1024]{0:T(1024)S(1)} %bitcast.307, ...), kind=kLoop, calls=%fused_computation.100 | loop fusion | flops 4718592 | bytes 5263360 | tf_op jit(solution)/shard_map/mul | solution.py:40
  126.6 1.6 copy.62
  128.2 0.2 divide_multiply_fusion.2
  128.5 0.4 fusion.114
  128.9 1.8 convolution_multiply_fusion.2
  130.7 1.3 copy.55
  132.0 0.7 bitcast_add_fusion.4
  132.7 1.0 fusion.60
  133.7 7.0 %fusion.62 = f32[1,1,256,16,64]{2,4,3,1,0:T(8,128)} fusion(f32[1,1,256,16,64]{2,4,3,1,0:T(8,128)S(1)} %fusion.60, f32[256,256]{1,0:T(8,128)S(1)} %fusion.114, f32[16,256]{1,0:T(8,128)S(1)} %bitcast_add_fusion.4, pred[256,256]{1,0:T(8,128)(4,1)S(1)} %copy-done.11, f32[256,16,64]{0,2,1:T(8,128)} %bitcast.288, f32[256,16]{0,1:T(8,128)S(1)} %copy-done.8), kind=kOutput, calls=%fused_computation.62 | convolution fusion | flops 810024960 | bytes 3506176 | tf_op jit(solution)/shard_map/bchij,bcjhp->bcihp/dot_general | solution.py:37
  140.7 1.6 copy.63
  142.4 4.7 %multiply_reduce_fusion = (f32[256]{0:T(256)S(1)}, f32[256,1024]{1,0:T(8,128)}) fusion(bf16[2,2048,1024]{2,1,0:T(8,128)(2,1)} %param.17, bf16[1,256,2048]{2,1,0:T(8,128)(2,1)S(1)} %get-tuple-element.10, f32[2048]{0:T(1024)S(1)} %bitcast.319, f32[256]{0:T(256)S(1)} %copy-done.40, f32[256,1024]{1,0:T(8,128)S(1)} %copy.63, ...), kind=kOutput, calls=%fused_computation.99 | convolution fusion | flops 1078722304 | bytes 8402944 | tf_op jit(solution)/shard_map/btd,de->bte/dot_general | solution.py:59
  147.0 5.8 %psum.30 = f32[1,256,1]{1,2,0:T(1,128)S(1)} all-reduce(f32[1,256,1]{1,2,0:T(1,128)S(1)} %bitcast.329), channel_id=1, replica_groups=mesh['dp'=2,'tp'=4] {'tp'}, use_global_device_ids=true, to_apply=%region_10.11 | all-reduce | flops 256 | bytes 2048 | tf_op jit(solution)/shard_map/psum | solution.py:71
  152.8 5.2 %fusion.33 = f32[1,256,2048]{2,1,0:T(8,128)} fusion(bf16[2,1024,2048]{2,1,0:T(8,128)(2,1)} %param.29, f32[256,1024]{1,0:T(8,128)} %get-tuple-element.48, f32[1024]{0:T(1024)S(1)} %bitcast.326, f32[256]{0:T(256)S(1)} %bitcast.331), kind=kOutput, calls=%fused_computation.37 | convolution fusion | flops 1074528256 | bytes 7345152 | tf_op jit(solution)/shard_map/bte,ed->btd/dot_general | solution.py:73
  158.0 46.3 %all-reduce.9.cloned.1.call-done = f32[1,256,2048]{2,1,0:T(8,128)} async-done(((f32[1,256,2048]{2,1,0:T(8,128)}), f32[1,256,2048]{2,1,0:T(8,128)}) %all-reduce.9.cloned.1.call-update) | async-done | bytes 2097168 | tf_op jit(solution)/shard_map/psum | solution.py:74
  204.3 2.8 %fusion.43 = bf16[1,256,2048]{2,1,0:T(8,128)(2,1)} fusion(f32[1,256,2048]{2,1,0:T(8,128)} %all-reduce.9.cloned.1.call-done, bf16[1,256,2048]{2,1,0:T(8,128)(2,1)S(1)} %get-tuple-element.10), kind=kLoop, calls=%fused_computation.45 | loop fusion | flops 1572864 | bytes 4194304 | tf_op jit(solution)/shard_map/convert_element_type | solution.py:75
  (117 shorter events, 1.2 us)
Async XLA Ops:
  6.5 103.1 %all-reduce.7.cloned.1.call-start = ((), (), s32[]{:S(2)}) async-start(), calls=%async_computation | async-start | bytes 4194304 | tf_op jit(solution)/shard_map/psum | solution.py:74
  7.9 20.3 %copy-start.25 = (f32[1,2048]{1,0:T(1,128)}, f32[1,2048]{1,0:T(1,128)S(1)}, u32[]{:S(2)}) copy-start(f32[1,2048]{1,0:T(1,128)S(1)} %get-tuple-element.24) | copy-start | bytes 24580
  9.4 18.8 %copy-start.37 = (f32[256]{0:T(256)}, f32[256]{0:T(256)S(1)}, u32[]{:S(2)}) copy-start(f32[256]{0:T(256)S(1)} %add_rsqrt_fusion.3) | copy-start | bytes 3076
  13.8 4.8 %copy-start.5 = (f32[256,16]{0,1:T(8,128)}, f32[256,16]{0,1:T(8,128)S(1)}, u32[]{:S(2)}) copy-start(f32[256,16]{0,1:T(8,128)S(1)} %compare_select_fusion.1) | copy-start | bytes 49156
  18.5 1.4 copy-start
  19.9 3.7 %copy-start.12 = (bf16[2,4,1024]{2,1,0:T(4,128)(2,1)S(1)}, bf16[2,4,1024]{2,1,0:T(4,128)(2,1)}, u32[]{:S(2)}) copy-start(bf16[2,4,1024]{2,1,0:T(4,128)(2,1)} %param.21) | copy-start | bytes 49156
  19.9 4.3 %copy-start.15 = (bf16[2,1024]{1,0:T(2,128)(2,1)S(1)}, bf16[2,1024]{1,0:T(2,128)(2,1)}, u32[]{:S(2)}) copy-start(bf16[2,1024]{1,0:T(2,128)(2,1)} %param.23) | copy-start | bytes 12292
  19.9 4.9 %copy-start.1 = (f32[1,256,1024]{2,1,0:T(8,128)S(1)}, f32[1,256,1024]{2,1,0:T(8,128)}, u32[]{:S(2)}) copy-start(f32[1,256,1024]{2,1,0:T(8,128)} %copy.52) | copy-start | bytes 3145732
  19.9 4.9 %copy-start.2 = (f32[1,256,1024]{2,1,0:T(8,128)S(1)}, f32[1,256,1024]{2,1,0:T(8,128)}, u32[]{:S(2)}) copy-start(f32[1,256,1024]{2,1,0:T(8,128)} %copy.50) | copy-start | bytes 3145732
  26.6 3.3 %copy-start.22 = (bf16[2,4,128]{2,1,0:T(4,128)(2,1)S(1)}, bf16[2,4,128]{2,1,0:T(4,128)(2,1)}, u32[]{:S(2)}) copy-start(bf16[2,4,128]{2,1,0:T(4,128)(2,1)} %param.22) | copy-start | bytes 6148
  26.6 3.9 %copy-start.35 = (bf16[2,128]{1,0:T(2,128)(2,1)S(1)}, bf16[2,128]{1,0:T(2,128)(2,1)}, u32[]{:S(2)}) copy-start(bf16[2,128]{1,0:T(2,128)(2,1)} %param.24) | copy-start | bytes 1540
  28.2 5.2 %copy-start.13 = (f32[1,1,256,16]{2,1,3,0:T(1,128)S(1)}, f32[1,1,256,16]{2,1,3,0:T(1,128)}, u32[]{:S(2)}) copy-start(f32[1,1,256,16]{2,1,3,0:T(1,128)} %get-tuple-element.11) | copy-start | bytes 49156
  33.4 1.3 copy-start.4
  33.4 2.3 %copy-start.9 = (f32[1,1,16,2,128]{4,3,2,1,0:T(2,128)S(1)}, f32[1,1,16,2,128]{4,3,2,1,0:T(2,128)}, u32[]{:S(2)}) copy-start(f32[1,1,16,2,128]{4,3,2,1,0:T(2,128)} %copy.48) | copy-start | bytes 49156
  33.4 2.3 %copy-start.6 = (f32[256,16]{0,1:T(8,128)S(1)}, f32[256,16]{0,1:T(8,128)}, u32[]{:S(2)}) copy-start(f32[256,16]{0,1:T(8,128)} %copy-done.5) | copy-start | bytes 49156
  33.4 2.3 %copy-start.10 = (pred[256,256]{1,0:T(8,128)(4,1)S(1)}, pred[256,256]{1,0:T(8,128)(4,1)}, u32[]{:S(2)}) copy-start(pred[256,256]{1,0:T(8,128)(4,1)} %iota_compare_fusion) | copy-start | bytes 196612
  42.8 1.6 copy-start.36
  42.8 1.8 copy-start.26
  42.8 1.8 copy-start.38
  44.6 13.4 %copy-start.16 = (bf16[2,1024]{1,0:T(2,128)(2,1)S(1)}, bf16[2,1024]{1,0:T(2,128)(2,1)}, u32[]{:S(2)}) copy-start(bf16[2,1024]{1,0:T(2,128)(2,1)} %param.28) | copy-start | bytes 12292
  63.8 140.5 %all-reduce.9.cloned.1.call-start = ((), (), s32[]{:S(2)}) async-start(), calls=%async_computation.1 | async-start | bytes 4194304 | tf_op jit(solution)/shard_map/psum | solution.py:74
  64.6 47.1 %copy-start.23 = (f32[1,2048]{1,0:T(1,128)S(1)}, f32[1,2048]{1,0:T(1,128)}, u32[]{:S(2)}) copy-start(f32[1,2048]{1,0:T(1,128)} %get-tuple-element.23) | copy-start | bytes 24580
  64.6 47.1 %copy-start.41 = (f32[16]{0:T(128)S(1)}, f32[16]{0:T(128)}, u32[]{:S(2)}) copy-start(f32[16]{0:T(128)} %get-tuple-element.42) | copy-start | bytes 196
  64.6 47.1 %copy-start.42 = (bf16[2,2048,16]{1,2,0:T(8,128)(2,1)S(1)}, bf16[2,2048,16]{1,2,0:T(8,128)(2,1)}, u32[]{:S(2)}) copy-start(bf16[2,2048,16]{1,2,0:T(8,128)(2,1)} %param.20) | copy-start | bytes 393220
  64.6 47.6 %copy-start.33 = (f32[16]{0:T(128)S(1)}, f32[16]{0:T(128)}, u32[]{:S(2)}) copy-start(f32[16]{0:T(128)} %get-tuple-element.39) | copy-start | bytes 196
  111.7 3.7 %copy-start.39 = (f32[256]{0:T(256)}, f32[256]{0:T(256)S(1)}, u32[]{:S(2)}) copy-start(f32[256]{0:T(256)S(1)} %add_rsqrt_fusion.1) | copy-start | bytes 3076
  112.2 9.2 %copy-start.7 = (f32[256,16]{0,1:T(8,128)}, f32[256,16]{0,1:T(8,128)S(1)}, u32[]{:S(2)}) copy-start(f32[256,16]{0,1:T(8,128)S(1)} %compare_select_fusion) | copy-start | bytes 49156
  121.4 1.4 copy-start.17
  121.4 1.4 copy-start.18
  121.4 1.4 copy-start.19
  121.4 1.4 copy-start.20
  121.4 1.4 copy-start.21
  126.6 1.6 copy-start.29
  126.6 1.6 copy-start.30
  126.6 1.6 copy-start.31
  126.6 1.6 copy-start.32
  126.6 1.6 copy-start.34
  128.2 2.5 %copy-start.14 = (f32[1,1,256,16]{2,1,3,0:T(1,128)S(1)}, f32[1,1,256,16]{2,1,3,0:T(1,128)}, u32[]{:S(2)}) copy-start(f32[1,1,256,16]{2,1,3,0:T(1,128)} %get-tuple-element.5) | copy-start | bytes 49156
  130.7 2.1 copy-start.3
  130.7 3.0 %copy-start.8 = (f32[256,16]{0,1:T(8,128)S(1)}, f32[256,16]{0,1:T(8,128)}, u32[]{:S(2)}) copy-start(f32[256,16]{0,1:T(8,128)} %copy-done.7) | copy-start | bytes 49156
  130.7 3.0 %copy-start.11 = (pred[256,256]{1,0:T(8,128)(4,1)S(1)}, pred[256,256]{1,0:T(8,128)(4,1)}, u32[]{:S(2)}) copy-start(pred[256,256]{1,0:T(8,128)(4,1)} %iota_compare_fusion) | copy-start | bytes 196612
  140.7 1.6 copy-start.24
  140.7 1.6 copy-start.27
  140.7 1.6 copy-start.40
  142.4 10.5 %copy-start.28 = (f32[1,1024]{1,0:T(1,128)S(1)}, f32[1,1024]{1,0:T(1,128)}, u32[]{:S(2)}) copy-start(f32[1,1024]{1,0:T(1,128)} %get-tuple-element.25) | copy-start | bytes 12292
Sparse Core Ops, SparseCore 0:
  63.9 45.7 all-reduce.6
  158.1 46.0 all-reduce.8
where the time goes:
time: 215 us; the launch traced here: 214 us
  waiting for transfers between devices  91.4 us (43%)
  matrix products  53.4 us (25%)
  other arithmetic  21.1 us (10%)
  local copies, waits for them, and re-layouts  19.6 us (9%)
  blocking collectives  14.5 us (7%)
  between operations  14 us (7%)
    psum x2, waiting for transfers between devices, mixer_layer(): full_out = lax.psum(part_out, 'tp')  91.3 us
    psum x2, blocking collectives, mixer_layer(): total_sq = lax.psum(part_sq, 'tp')  14.5 us
    dot_general x2, matrix products, ssd_blocks(): jnp.einsum('bchij,bcjhp->bcihp', mix_mat, x_dt, precision=FULL_PRECISION)  14.1 us
    dot_general x2, matrix products, mixer_layer(): jnp.einsum('bte,ed->btd', normed_y, w_out, preferred_element_type=jnp.flo...  10.3 us
    dot_general x2, matrix products, mixer_layer(): jnp.einsum('btd,de->bte', normed, w_z, preferred_element_type=jnp.float32)  9.37 us
    dot_general x2, matrix products, mixer_layer(): jnp.einsum('btd,de->bte', normed, w_x, preferred_element_type=jnp.float32)  7.92 us
    mul x2, other arithmetic, ssd_blocks(): x_dt * tail_decay[..., None]  5.52 us
    mul x6, local copies, waits for them, and re-layouts, ssd_blocks(): x_dt * tail_decay[..., None]  4.93 us
  transfers between devices with their start and end apart: 2, of which 2 were waited for; matrix products, arithmetic and copies ran while one was open for 0% of the time, Pallas kernels for 0%

commit v1 on v0

v1 whole, which is shorter than its diff:
```python
import functools

import jax
import jax.numpy as jnp
from jax import lax
from jax.experimental import pallas as pl
from jax.experimental.pallas import tpu as pltpu
from jax.sharding import PartitionSpec as P

EPSILON = 1e-5
MESH = pl.DeviceIdType.MESH
CHUNK = 64
PIECE = 256
EXTRA = 8
HEAD = 64
F32 = jnp.float32
BF16 = jnp.bfloat16


def split3(val):
    hi = val.astype(BF16).astype(F32)
    rest = val - hi
    mid = rest.astype(BF16).astype(F32)
    return hi, mid, rest - mid


def stack3(val):
    return jnp.concatenate(split3(val), axis=0).astype(BF16)


def dot(a, b):
    return lax.dot_general(a, b, (((1,), (0,)), ((), ())), preferred_element_type=F32)


def dot_nt(a, b):
    return lax.dot_general(a, b, (((1,), (1,)), ((), ())), preferred_element_type=F32)


def exact_dot(a_stack, b_parts, product=dot):
    rows = a_stack.shape[0] // 3
    b_hi, b_mid, b_lo = b_parts
    r1 = product(a_stack, b_hi)
    r2 = product(a_stack[: 2 * rows], b_mid)
    r3 = product(a_stack[:rows], b_lo)
    small = r1[2 * rows :] + r2[rows:] + r3
    return r1[:rows] + (r1[rows : 2 * rows] + r2[:rows] + small)


def iota(shape, dim):
    return lax.broadcasted_iota(jnp.int32, shape, dim)


def kernel(inner, hid_h, nw_h, wz_h, wx_h, wbc_h, wdt_h, cx_h, cbc_h, bx_h, bbc_h, dtb_h, al_h, ds_h, gw_h, wo_h,
           out_ref, hid, nw, wz, wx, wbc, wdt, cx, cbc, bx, bbc, dtb, al, ds, gw, wo,
           ubuf, psend, prcv, qbuf, own, hbuf, x0s, q0s, xs, vs, state, gbuf,
           small_sem, hid_sem, w_sem, ps_sem, pr_sem, qs_sem, qr_sem, us_sem, ur_sem):
    me = lax.axis_index("tp")
    core = me % 2
    chip = me // 2
    peer = me + 1 - 2 * core
    cross = (me + 2) % 4
    n_chunks = hid_h.shape[1] // CHUNK
    n_piece = wx_h.shape[2] // PIECE
    layers = nw_h.shape[0]
    local = wx_h.shape[2]
    half = wo_h.shape[2] // 2

    barrier = pltpu.get_barrier_semaphore()
    for other in (peer, cross):
        pl.semaphore_signal(barrier, inc=1, device_id={"tp": other}, device_id_type=MESH)

    smalls = [pltpu.make_async_copy(src, dst, small_sem.at[i]) for i, (src, dst) in enumerate(
        [(nw_h, nw), (cx_h, cx), (cbc_h, cbc), (bx_h, bx), (bbc_h, bbc), (dtb_h, dtb), (al_h, al), (ds_h, ds), (gw_h, gw), (wdt_h, wdt)])]

    def hid_copy(c):
        return pltpu.make_async_copy(hid_h.at[0, pl.ds(c * CHUNK, CHUNK)], hid.at[c], hid_sem.at[c])

    def weight_copies(layer):
        cols = lambda n: pl.ds(n * PIECE, PIECE)
        bc = pltpu.make_async_copy(wbc_h.at[layer], wbc.at[layer], w_sem.at[layer, 0])
        xcp = [pltpu.make_async_copy(wx_h.at[layer, :, cols(n)], wx.at[layer, n], w_sem.at[layer, 1 + n]) for n in range(n_piece)]
        zcp = [pltpu.make_async_copy(wz_h.at[layer, :, cols(n)], wz.at[layer, n], w_sem.at[layer, 5 + n]) for n in range(n_piece)]
        ocp = []
        for side in range(2):
            for n in range(n_piece):
                ocp.append(pltpu.make_async_copy(wo_h.at[layer, :, cols(side * n_piece + n)], wo.at[layer, side, n], w_sem.at[layer, 9 + side * n_piece + n]))
        return bc, xcp, zcp, ocp

    hid_copy(0).start()
    for cp in smalls:
        cp.start()
    first_w = weight_copies(0)
    first_w[0].start()
    for group in first_w[1:]:
        for cp in group:
            cp.start()
    for c in range(1, n_chunks):
        hid_copy(c).start()

    def rows_of(m):
        return CHUNK + EXTRA if m == 0 else CHUNK

    def p_copy(s, m):
        part = pl.ds(0, rows_of(m))
        return pltpu.make_async_remote_copy(src_ref=psend.at[s, m, part], dst_ref=prcv.at[s, m, part], send_sem=ps_sem.at[s, m],
                                            recv_sem=pr_sem.at[s, m], device_id={"tp": peer}, device_id_type=MESH)

    def q_copy(s, m):
        part = pl.ds(0, rows_of(m))
        return pltpu.make_async_remote_copy(src_ref=qbuf.at[chip, s, m, part], dst_ref=qbuf.at[chip, s, m, part], send_sem=qs_sem.at[s, m],
                                            recv_sem=qr_sem.at[s, m], device_id={"tp": cross}, device_id_type=MESH)

    def u_copy(layer, c, m):
        s = layer * n_chunks + c
        return pltpu.make_async_remote_copy(src_ref=ubuf.at[layer + 1, core, c, m], dst_ref=ubuf.at[layer + 1, core, c, m], send_sem=us_sem.at[s, m],
                                            recv_sem=ur_sem.at[s, m], device_id={"tp": peer}, device_id_type=MESH)

    row64 = iota((CHUNK, PIECE), 0)
    lane64 = iota((CHUNK, PIECE), 1) % HEAD
    eye = row64 == lane64
    causal = row64 >= lane64
    low_head = iota((CHUNK, 128), 1) < HEAD

    def to_row(col):
        return jnp.sum(jnp.where(eye, col, 0.0), axis=0, keepdims=True)

    def to_col(row):
        return jnp.sum(jnp.where(eye[:, :HEAD], row[:, :HEAD], 0.0), axis=1, keepdims=True)

    def scale_of(square_sum):
        return lax.rsqrt(square_sum / inner + EPSILON) * (1.0 / 64.0)

    def inverse_of(square_sum):
        return jnp.where(square_sum < jnp.inf, 64.0 * jnp.sqrt(square_sum / inner + EPSILON), 0.0)

    def head_blocks(part):
        left, right = part[:, :128], part[:, 128:]
        none = jnp.zeros_like(left)
        rows = [jnp.concatenate([jnp.where(low_head, left, 0.0), none], axis=1), jnp.concatenate([jnp.where(low_head, 0.0, left), none], axis=1),
                jnp.concatenate([none, jnp.where(low_head, right, 0.0)], axis=1), jnp.concatenate([none, jnp.where(low_head, 0.0, right)], axis=1)]
        return jnp.concatenate(rows, axis=0).astype(BF16)

    def start_layer():
        state[...] = jnp.zeros_like(state)
        x0s[0:8] = jnp.zeros((8, local), F32)
        q0s[0:8] = jnp.zeros((8, q0s.shape[1]), F32)

    def tap_sum(buf, lanes, kern, bias):
        total = bias
        for j in range(4):
            total = total + buf[5 + j : 5 + j + CHUNK, lanes] * kern[j : j + 1].astype(F32)
        return total

    def step(layer, c, waits=None):
        s = layer * n_chunks + c
        bc_wait, x_wait, z_wait, o_wait = waits if waits is not None else (None, None, None, None)
        square = jnp.zeros((CHUNK, 1), F32)
        for side in range(2):
            for m in range(n_piece):
                val = ubuf[layer, side, c, m]
                square = square + jnp.sum(val * val, axis=1, keepdims=True)
        scale = lax.rsqrt(square / (2 * half) + EPSILON)
        norm_row = nw[layer : layer + 1].astype(F32)
        for side in range(2):
            for m in range(n_piece):
                at = side * half + m * PIECE
                hbuf[:, at : at + PIECE] = (ubuf[layer, side, c, m] * scale * norm_row[:, at : at + PIECE]).astype(BF16)
        if waits is not None:
            bc_wait.wait()
        q0s[8:, :] = dot(hbuf[...], wbc[layer]).astype(BF16).astype(F32)
        bc = jax.nn.silu(tap_sum(q0s, slice(None), cbc[layer], bbc[layer : layer + 1].astype(F32)))
        q0s[0:8] = q0s[CHUNK : CHUNK + 8]
        wdt3 = jnp.concatenate([wdt[layer]] * 3, axis=0)
        r_pre = dot_nt(hbuf[...], wdt3).astype(BF16).astype(F32)
        triple = lambda ref: jnp.concatenate([ref[layer : layer + 1]] * 3, axis=1)
        dt_in = r_pre + triple(dtb)
        dt_val = jnp.maximum(dt_in, 0.0) + jnp.log1p(jnp.exp(-jnp.abs(dt_in)))
        a_vals = -dt_val * jnp.exp(triple(al))
        tri = (iota((CHUNK, 3 * CHUNK), 0) >= iota((CHUNK, 3 * CHUNK), 1) % CHUNK).astype(F32).astype(BF16)
        a_cum = dot(tri, stack3(a_vals))
        skip = jnp.broadcast_to(triple(ds), (8, a_cum.shape[1]))
        to_spread = jnp.concatenate([dt_val, a_cum, skip], axis=0)
        hi, mid, lo = split3(to_spread)
        lane = iota(to_spread.shape, 1)
        n_heads = local // HEAD
        spread_in = jnp.where(lane < n_heads, hi, jnp.where(lane < 2 * n_heads, mid, lo)).astype(BF16)

        swapped = pltpu.roll(bc, HEAD, 1)
        c_stack = stack3(swapped[:, :HEAD])
        b_parts = split3(bc[:, :HEAD])
        cb = exact_dot(c_stack, [jnp.concatenate([part] * 4, axis=0).astype(BF16) for part in b_parts], dot_nt)
        bt_stack = stack3(jnp.transpose(bc)[:HEAD])

        gate_sq = jnp.zeros((CHUNK, 1), F32)
        for n in range(n_piece):
            at = slice(n * PIECE, (n + 1) * PIECE)
            if waits is not None:
                x_wait[n].wait()
            x0s[8:, at] = dot(hbuf[...], wx[layer, n]).astype(BF16).astype(F32)
            x_act = jax.nn.silu(tap_sum(x0s, at, cx[layer, :, at], bx[layer : layer + 1, at].astype(F32)))
            x0s[0:8, at] = x0s[CHUNK : CHUNK + 8, at]
            group = n * (PIECE // HEAD)
            pick = (iota((3 * n_heads, PIECE), 1) // HEAD + group == iota((3 * n_heads, PIECE), 0) % n_heads).astype(F32).astype(BF16)
            spread = dot(spread_in, pick)
            dt_e, a_e, skip_e = spread[:CHUNK], spread[CHUNK : 2 * CHUNK], spread[2 * CHUNK : 2 * CHUNK + 1]
            a_row = to_row(a_e)
            a_last = a_e[CHUNK - 1 : CHUNK]
            decay = jnp.where(causal, jnp.exp(jnp.minimum(a_e - a_row, 0.0)), 0.0) * cb
            x_dt = x_act * dt_e
            y = exact_dot(stack3(decay), [head_blocks(part) for part in split3(x_dt)])
            old = state[:, at]
            carried = exact_dot(c_stack, [part.astype(BF16) for part in split3(old)])
            y = y + carried * jnp.exp(a_e) + skip_e * x_act
            tail = x_dt * jnp.exp(a_last - a_e)
            state[:, at] = jnp.exp(a_last) * old + exact_dot(bt_stack, [part.astype(BF16) for part in split3(tail)])
            xs[:, at] = y
        for n in range(n_piece):
            at = slice(n * PIECE, (n + 1) * PIECE)
            if waits is not None:
                z_wait[n].wait()
            z = dot(hbuf[...], wz[layer, n]).astype(BF16).astype(F32)
            v = xs[:, at] * jax.nn.silu(z)
            vs[:, at] = v
            gate_sq = gate_sq + jnp.sum(v * v, axis=1, keepdims=True)
        scale = scale_of(gate_sq)
        gbuf[...] = (vs[...] * scale * gw[layer : layer + 1].astype(F32)).astype(BF16)
        psend[s, 0, CHUNK:] = jnp.broadcast_to(to_row(gate_sq), (EXTRA, PIECE))
        if waits is not None:
            for cp in o_wait:
                cp.wait()
            pl.semaphore_wait(barrier, 2)
        for m in range(n_piece):
            psend[s, m, 0:CHUNK] = dot(gbuf[...], wo[layer, 1 - core, m])
            p_copy(s, m).start()
        for m in range(n_piece):
            own[m] = dot(gbuf[...], wo[layer, core, m])
        for m in range(n_piece):
            p_copy(s, m).wait_recv()
            if m == 0:
                peer_sq = to_col(prcv[s, 0, CHUNK : CHUNK + 1])
                chip_sq = gate_sq + peer_sq
                chip_scale = scale_of(chip_sq)
                f_own = chip_scale * inverse_of(gate_sq)
                f_peer = chip_scale * inverse_of(peer_sq)
                qbuf[chip, s, 0, CHUNK:] = jnp.broadcast_to(to_row(chip_sq), (EXTRA, PIECE))
            qbuf[chip, s, m, 0:CHUNK] = own[m] * f_own + prcv[s, m, 0:CHUNK] * f_peer
            q_copy(s, m).start()

    def finish(layer, c, last):
        s = layer * n_chunks + c
        for m in range(n_piece):
            q_copy(s, m).wait_recv()
            if m == 0:
                sq0 = to_col(qbuf[0, s, 0, CHUNK : CHUNK + 1])
                sq1 = to_col(qbuf[1, s, 0, CHUNK : CHUNK + 1])
                norm = lax.rsqrt((sq0 + sq1) / inner + EPSILON)
                f0 = norm * inverse_of(sq0)
                f1 = norm * inverse_of(sq1)
            total = ubuf[layer, core, c, m] + (qbuf[0, s, m, 0:CHUNK] * f0 + qbuf[1, s, m, 0:CHUNK] * f1)
            new = total.astype(BF16)
            ubuf[layer + 1, core, c, m] = new.astype(F32)
            u_copy(layer, c, m).start()
            if last:
                out_ref[0, pl.ds(c * CHUNK, CHUNK), pl.ds(pl.multiple_of(core * half + m * PIECE, PIECE), PIECE)] = new
        for m in range(n_piece):
            u_copy(layer, c, m).wait_recv()
            if last:
                out_ref[0, pl.ds(c * CHUNK, CHUNK), pl.ds(pl.multiple_of((1 - core) * half + m * PIECE, PIECE), PIECE)] = ubuf[layer + 1, 1 - core, c, m].astype(BF16)

    def load_hidden(c):
        hid_copy(c).wait()
        for side in range(2):
            for m in range(n_piece):
                at = side * half + m * PIECE
                ubuf[0, side, c, m] = hid[c, :, at : at + PIECE].astype(F32)

    start_layer()
    load_hidden(0)
    for cp in smalls:
        cp.wait()
    step(0, 0, first_w)
    later = [weight_copies(layer) for layer in range(1, layers)]
    for groups in later:
        groups[0].start()
        for group in groups[1:]:
            for cp in group:
                cp.start()

    @pl.loop(1, n_chunks)
    def _(c):
        load_hidden(c)
        step(0, c)

    for layer in range(1, layers):
        start_layer()
        groups = later[layer - 1]
        groups[0].wait()
        for group in groups[1:]:
            for cp in group:
                cp.wait()

        @pl.loop(0, n_chunks)
        def _(c):
            finish(layer - 1, c, False)
            step(layer, c)

    @pl.loop(0, n_chunks)
    def _(c):
        finish(layers - 1, c, True)

    @pl.loop(0, layers * n_chunks)
    def _(s):
        for m in range(n_piece):
            p_copy(s, m).wait_send()
            q_copy(s, m).wait_send()
            u_copy(s // n_chunks, s % n_chunks, m).wait_send()


def solution(mesh):
    in_specs = (P('dp'), P(), P(None, None, 'tp'), P(None, None, 'tp'), P(), P(None, None, 'tp'), P(None, None, 'tp'), P(), P(None, 'tp'), P(),
                P(None, 'tp'), P(None, 'tp'), P(None, 'tp'), P(None, 'tp'), P(None, 'tp', None))
    tp_size = mesh.shape['tp']

    def device_forward(hidden, norm_w, w_z, w_x, w_bc, w_dt, conv_x, conv_bc, bias_x, bias_bc, dt_bias, a_log, d_skip, gate_w, w_out):
        layers, width, local = w_x.shape
        n_chunks = hidden.shape[1] // CHUNK
        n_piece = local // PIECE
        steps = layers * n_chunks
        bc_width = w_bc.shape[-1]
        w_dt = jnp.swapaxes(w_dt, 1, 2)
        vm = lambda shape, dtype: pltpu.VMEM(shape, dtype)
        same = lambda arr: pltpu.VMEM(arr.shape, arr.dtype)
        scratch = [
            vm((n_chunks, CHUNK, width), BF16), same(norm_w), vm((layers, n_piece, width, PIECE), BF16), vm((layers, n_piece, width, PIECE), BF16),
            same(w_bc), same(w_dt), same(conv_x), same(conv_bc), same(bias_x), same(bias_bc), same(dt_bias), same(a_log), same(d_skip), same(gate_w),
            vm((layers, 2, n_piece, local, PIECE), BF16),
            vm((layers + 1, 2, n_chunks, n_piece, CHUNK, PIECE), F32),
            vm((steps, n_piece, CHUNK + EXTRA, PIECE), F32), vm((steps, n_piece, CHUNK + EXTRA, PIECE), F32),
            vm((2, steps, n_piece, CHUNK + EXTRA, PIECE), F32),
            vm((n_piece, CHUNK, PIECE), F32), vm((CHUNK, width), BF16), vm((CHUNK + 8, local), F32), vm((CHUNK + 8, bc_width), F32),
            vm((CHUNK, local), F32), vm((CHUNK, local), F32), vm((HEAD, local), F32), vm((CHUNK, local), BF16),
            pltpu.SemaphoreType.DMA((10,)), pltpu.SemaphoreType.DMA((n_chunks,)), pltpu.SemaphoreType.DMA((layers, 9 + 2 * n_piece)),
        ] + [pltpu.SemaphoreType.DMA((steps, n_piece)) for _ in range(6)]
        return pl.pallas_call(
            functools.partial(kernel, float(local * tp_size)),
            out_shape=jax.ShapeDtypeStruct(hidden.shape, hidden.dtype),
            in_specs=[pl.BlockSpec(memory_space=pl.ANY)] * 15,
            out_specs=pl.BlockSpec(memory_space=pltpu.VMEM),
            scratch_shapes=scratch,
            compiler_params=pltpu.CompilerParams(collective_id=0, has_side_effects=True, vmem_limit_bytes=60 * 1024 * 1024),
        )(hidden, norm_w, w_z, w_x, w_bc, w_dt, conv_x, conv_bc, bias_x, bias_bc, dt_bias, a_log, d_skip, gate_w, w_out)

    return jax.shard_map(device_forward, mesh=mesh, in_specs=in_specs, out_specs=P('dp'), check_vma=False)
```

time: 215 us -> 79.2 us (0.37)
  waiting for transfers between devices: 91.4 us -> 0 us
  Pallas kernels: 0 us -> 76.8 us
  matrix products: 53.4 us -> 0 us
  other arithmetic: 21.1 us -> 0 us
  local copies, waits for them, and re-layouts: 19.6 us -> 2.3 us
  blocking collectives: 14.5 us -> 0 us
  between operations: 14 us -> 0.01 us
    psum x2 -> x0, waiting for transfers between devices: 91.3 us -> none  [mixer_layer(): full_out = lax.psum(part_out, 'tp')]
    pallas_call x0 -> x1, Pallas kernels: none -> 76.8 us  [device_forward(): pl.pallas_call(functools.partial(kernel, float(local * tp_size)), out_sha...]
    dot_general x18 -> x0, matrix products: 53.4 us -> none  [the longest x2 14.1 us: ssd_blocks(): jnp.einsum('bchij,bcjhp->bcihp', mix_mat, x_dt, precision=FULL_PRECISION)]
    psum x2 -> x0, blocking collectives: 14.5 us -> none  [mixer_layer(): total_sq = lax.psum(part_sq, 'tp')]
    mul x17 -> x0, local copies, waits for them, and re-layouts: 11.2 us -> none  [the longest x6 4.93 us: ssd_blocks(): x_dt * tail_decay[..., None]]
    mul x6 -> x0, other arithmetic: 7.19 us -> none  [the longest x2 5.52 us: ssd_blocks(): x_dt * tail_decay[..., None]]
    convert_element_type x5 -> x0, other arithmetic: 5.99 us -> none  [the longest x1 2.85 us: mixer_layer(): return (residual + full_out).astype(jnp.bfloat16)]
    reduce_sum x2 -> x0, other arithmetic: 3.49 us -> none  [mixer_layer(): jnp.mean(residual * residual, axis=-1, keepdims=True) + EPSILON]
  transfers between devices with their start and end apart: 2 -> 0, of which waited for: 2 -> 0; matrix products, arithmetic and copies ran while one was open for 0% -> 0% of each run, Pallas kernels for 0% -> 0%
where the time goes in v1:
time: 79.2 us; the launch traced here: 79.1 us
  Pallas kernels  76.8 us (97%)
  local copies, waits for them, and re-layouts  2.3 us (3%)
    pallas_call x1, Pallas kernels, device_forward(): pl.pallas_call(functools.partial(kernel, float(local * tp_size)), out_sha...  76.8 us
    unnamed x1, local copies, waits for them, and re-layouts  2.3 us

profile of v1, /device:TPU:0, one launch (start us, length us, event | category | flops | bytes accessed | tf_op | source)
XLA Modules:
  0.0 79.1 jit_solution(13801022374651459549)
XLA Ops:
  0.0 76.8 %shard_map.145 = bf16[1,256,2048]{2,1,0:T(8,128)(2,1)} custom-call(bf16[1,256,2048]{2,1,0:T(8,128)(2,1)} %hid_h.1, bf16[2,2048]{1,0:T(2,128)(2,1)} %nw_h.1, bf16[2,2048,1024]{2,1,0:T(8,128)(2,1)} %wz_h.1, bf16[2,2048,1024]{2,1,0:T(8,128)(2,1)} %wx_h.1, bf16[2,2048,128]{2,1,0:T(8,128)(2,1)} %wbc_h.1, bf16[2,16,2048]{2,1,0:T(8,128)(2,1)} %bitcast.1, ...), custom_call_target="tpu_custom_call" | custom-call | tf_op jit(solution)/shard_map/pallas_call | solution.py:344
  76.8 2.3 %copy.17 = bf16[1,256,2048]{2,1,0:T(8,128)(2,1)} copy(bf16[1,256,2048]{2,1,0:T(8,128)(2,1)} %shard_map.145) | data formatting | bytes 2097152

commit v2 on v1

v2 whole, which is shorter than its diff:
```python
import functools

import jax
import jax.numpy as jnp
from jax import lax
from jax.experimental import pallas as pl
from jax.experimental.pallas import tpu as pltpu
from jax.sharding import PartitionSpec as P

EPSILON = 1e-5
MESH = pl.DeviceIdType.MESH
CHUNK = 128
SUB = 64
PIECE = 256
EXTRA = 8
HEAD = 64
F32 = jnp.float32
BF16 = jnp.bfloat16


def split3(val):
    hi = val.astype(BF16).astype(F32)
    rest = val - hi
    mid = rest.astype(BF16).astype(F32)
    return hi, mid, rest - mid


def stack3(val):
    return jnp.concatenate(split3(val), axis=0).astype(BF16)


def dot(a, b):
    return lax.dot_general(a, b, (((1,), (0,)), ((), ())), preferred_element_type=F32)


def dot_nt(a, b):
    return lax.dot_general(a, b, (((1,), (1,)), ((), ())), preferred_element_type=F32)


def exact_dot(a_stack, b_parts, product=dot):
    rows = a_stack.shape[0] // 3
    b_hi, b_mid, b_lo = b_parts
    r1 = product(a_stack, b_hi)
    r2 = product(a_stack[: 2 * rows], b_mid)
    r3 = product(a_stack[:rows], b_lo)
    small = r1[2 * rows :] + r2[rows:] + r3
    return r1[:rows] + (r1[rows : 2 * rows] + r2[:rows] + small)


def iota(shape, dim):
    return lax.broadcasted_iota(jnp.int32, shape, dim)


def kernel(inner, hid_h, nw_h, wz_h, wx_h, wbc_h, wdt_h, cx_h, cbc_h, bx_h, bbc_h, dtb_h, al_h, ds_h, gw_h, wo_h,
           out_ref, hid, nw, wz, wx, wbc, wdt, cx, cbc, bx, bbc, dtb, al, ds, gw, wo,
           ubuf, psend, prcv, qbuf, own, hbuf, x0s, q0s, xs, ys, spread, state, gbuf,
           small_sem, hid_sem, w_sem, ps_sem, pr_sem, qs_sem, qr_sem, us_sem, ur_sem):
    me = lax.axis_index("tp")
    core = me % 2
    chip = me // 2
    peer = me + 1 - 2 * core
    cross = (me + 2) % 4
    n_chunks = hid_h.shape[1] // CHUNK
    subs = CHUNK // SUB
    n_subs = n_chunks * subs
    n_piece = wx_h.shape[2] // PIECE
    layers = nw_h.shape[0]
    local = wx_h.shape[2]
    half = wo_h.shape[2] // 2

    barrier = pltpu.get_barrier_semaphore()
    for other in (peer, cross):
        pl.semaphore_signal(barrier, inc=1, device_id={"tp": other}, device_id_type=MESH)

    smalls = [pltpu.make_async_copy(src, dst, small_sem.at[i]) for i, (src, dst) in enumerate(
        [(nw_h, nw), (cx_h, cx), (cbc_h, cbc), (bx_h, bx), (bbc_h, bbc), (dtb_h, dtb), (al_h, al), (ds_h, ds), (gw_h, gw), (wdt_h, wdt)])]

    def hid_copy(c):
        return pltpu.make_async_copy(hid_h.at[0, pl.ds(c * SUB, SUB)], hid.at[c], hid_sem.at[c])

    def weight_copies(layer):
        cols = lambda n: pl.ds(n * PIECE, PIECE)
        bc = pltpu.make_async_copy(wbc_h.at[layer], wbc.at[layer], w_sem.at[layer, 0])
        xcp = [pltpu.make_async_copy(wx_h.at[layer, :, cols(n)], wx.at[layer, n], w_sem.at[layer, 1 + n]) for n in range(n_piece)]
        zcp = [pltpu.make_async_copy(wz_h.at[layer, :, cols(n)], wz.at[layer, n], w_sem.at[layer, 5 + n]) for n in range(n_piece)]
        ocp = []
        for side in range(2):
            for n in range(n_piece):
                ocp.append(pltpu.make_async_copy(wo_h.at[layer, :, cols(side * n_piece + n)], wo.at[layer, side, n], w_sem.at[layer, 9 + side * n_piece + n]))
        return bc, xcp, zcp, ocp

    for r in range(subs):
        hid_copy(r).start()
    for cp in smalls:
        cp.start()
    bc_cp, x_cp, z_cp, o_cp = weight_copies(0)
    bc_cp.start()
    x_cp[0].start()
    x_cp[1].start()
    for r in range(subs, n_subs):
        hid_copy(r).start()

    def rows_of(m):
        return SUB + EXTRA if m == 0 else SUB

    def p_copy(s, m):
        part = pl.ds(0, rows_of(m))
        return pltpu.make_async_remote_copy(src_ref=psend.at[s, m, part], dst_ref=prcv.at[s, m, part], send_sem=ps_sem.at[s, m],
                                            recv_sem=pr_sem.at[s, m], device_id={"tp": peer}, device_id_type=MESH)

    def q_copy(s, m):
        part = pl.ds(0, rows_of(m))
        return pltpu.make_async_remote_copy(src_ref=qbuf.at[chip, s, m, part], dst_ref=qbuf.at[chip, s, m, part], send_sem=qs_sem.at[s, m],
                                            recv_sem=qr_sem.at[s, m], device_id={"tp": cross}, device_id_type=MESH)

    def u_copy(s, m):
        layer, c = s // n_subs, s % n_subs
        return pltpu.make_async_remote_copy(src_ref=ubuf.at[layer + 1, core, c, m], dst_ref=ubuf.at[layer + 1, core, c, m], send_sem=us_sem.at[s, m],
                                            recv_sem=ur_sem.at[s, m], device_id={"tp": peer}, device_id_type=MESH)

    row64 = iota((SUB, PIECE), 0)
    lane64 = iota((SUB, PIECE), 1) % HEAD
    eye = row64 == lane64
    causal = row64 >= lane64
    low_head = iota((SUB, 128), 1) < HEAD

    def to_row(col):
        return jnp.sum(jnp.where(eye, col, 0.0), axis=0, keepdims=True)

    def to_col(row):
        return jnp.sum(jnp.where(eye[:, :HEAD], row[:, :HEAD], 0.0), axis=1, keepdims=True)

    def scale_of(square_sum):
        return lax.rsqrt(square_sum / inner + EPSILON) * (1.0 / 64.0)

    def inverse_of(square_sum):
        return jnp.where(square_sum < jnp.inf, 64.0 * jnp.sqrt(square_sum / inner + EPSILON), 0.0)

    def head_blocks(part):
        left, right = part[:, :128], part[:, 128:]
        none = jnp.zeros_like(left)
        rows = [jnp.concatenate([jnp.where(low_head, left, 0.0), none], axis=1), jnp.concatenate([jnp.where(low_head, 0.0, left), none], axis=1),
                jnp.concatenate([none, jnp.where(low_head, right, 0.0)], axis=1), jnp.concatenate([none, jnp.where(low_head, 0.0, right)], axis=1)]
        return jnp.concatenate(rows, axis=0).astype(BF16)

    def row_of(ref, layer, lanes=slice(None)):
        row = ref[0:1, lanes]
        for at in range(1, layers):
            row = jnp.where(layer == at, ref[at : at + 1, lanes], row)
        return row.astype(F32)

    def start_layer():
        state[...] = jnp.zeros_like(state)
        x0s[0:8] = jnp.zeros((8, local), F32)
        q0s[0:8] = jnp.zeros((8, q0s.shape[1]), F32)

    def tap_sum(buf, lanes, kern, bias):
        total = bias
        for j in range(4):
            total = total + buf[5 + j : 5 + j + CHUNK, lanes] * kern[j : j + 1].astype(F32)
        return total

    def head(layer, c, first):
        square = [jnp.zeros((SUB, 1), F32) for _ in range(subs)]
        for r in range(subs):
            for side in range(2):
                for m in range(n_piece):
                    val = ubuf[layer, side, subs * c + r, m]
                    square[r] = square[r] + jnp.sum(val * val, axis=1, keepdims=True)
        norm_row = row_of(nw, layer)
        for r in range(subs):
            scale = lax.rsqrt(square[r] / (2 * half) + EPSILON)
            for side in range(2):
                for m in range(n_piece):
                    at = side * half + m * PIECE
                    hbuf[r * SUB : (r + 1) * SUB, at : at + PIECE] = (ubuf[layer, side, subs * c + r, m] * scale * norm_row[:, at : at + PIECE]).astype(BF16)
        if first:
            bc_cp.wait()
            x_cp[2].start()
            x_cp[3].start()
        q0s[8:, :] = dot(hbuf[...], wbc[layer]).astype(BF16).astype(F32)
        wdt3 = jnp.concatenate([wdt[layer]] * 3, axis=0)
        r_pre = dot_nt(hbuf[...], wdt3).astype(BF16).astype(F32)
        for n in range(n_piece):
            at = slice(n * PIECE, (n + 1) * PIECE)
            if first and n % 2 == 0:
                x_cp[n].wait()
                x_cp[n + 1].wait()
                for cp in z_cp if n == 0 else o_cp:
                    cp.start()
            x0s[8:, at] = dot(hbuf[...], wx[layer, n]).astype(BF16).astype(F32)
        bc = jax.nn.silu(tap_sum(q0s, slice(None), cbc[layer], row_of(bbc, layer)))
        q0s[0:8] = q0s[CHUNK : CHUNK + 8]
        triple = lambda ref: jnp.concatenate([row_of(ref, layer)] * 3, axis=1)
        dt_in = r_pre + triple(dtb)
        dt_val = jnp.maximum(dt_in, 0.0) + jnp.log1p(jnp.exp(-jnp.abs(dt_in)))
        a_vals = -dt_val * jnp.exp(triple(al))
        to_t, from_t = iota((CHUNK, 3 * CHUNK), 0), iota((CHUNK, 3 * CHUNK), 1) % CHUNK
        tri = jnp.where((to_t >= from_t) & (to_t // SUB == from_t // SUB), 1.0, 0.0).astype(BF16)
        a_cum = dot(tri, stack3(a_vals))
        skip = jnp.broadcast_to(triple(ds), (8, a_cum.shape[1]))
        to_spread = jnp.concatenate([dt_val, a_cum, skip], axis=0)
        hi, mid, lo = split3(to_spread)
        lane = iota(to_spread.shape, 1)
        n_heads = local // HEAD
        spread_in = jnp.where(lane < n_heads, hi, jnp.where(lane < 2 * n_heads, mid, lo)).astype(BF16)
        for n in range(n_piece):
            at = slice(n * PIECE, (n + 1) * PIECE)
            group = n * (PIECE // HEAD)
            pick = jnp.where(iota((3 * n_heads, PIECE), 1) // HEAD + group == iota((3 * n_heads, PIECE), 0) % n_heads, 1.0, 0.0).astype(BF16)
            spread[:, at] = dot(spread_in, pick)
        swapped = pltpu.roll(bc, HEAD, 1)
        turned = jnp.transpose(bc)
        c_stack, bt_stack, cb = [], [], []
        for r in range(subs):
            rows = slice(r * SUB, (r + 1) * SUB)
            c_stack.append(stack3(swapped[rows, :HEAD]))
            bt_stack.append(stack3(turned[:HEAD, rows]))
            cb.append(exact_dot(c_stack[r], [jnp.concatenate([part] * 4, axis=0).astype(BF16) for part in split3(bc[rows, :HEAD])], dot_nt))
        for n in range(n_piece):
            at = slice(n * PIECE, (n + 1) * PIECE)
            xs[:, at] = jax.nn.silu(tap_sum(x0s, at, cx[layer, :, at], row_of(bx, layer, at)))
            x0s[0:8, at] = x0s[CHUNK : CHUNK + 8, at]
        for r in range(subs):
            rows = slice(r * SUB, (r + 1) * SUB)
            for n in range(n_piece):
                at = slice(n * PIECE, (n + 1) * PIECE)
                a_e = spread[CHUNK + r * SUB : CHUNK + (r + 1) * SUB, at]
                decay = jnp.where(causal, jnp.exp(jnp.minimum(a_e - to_row(a_e), 0.0)), 0.0) * cb[r]
                x_dt = xs[rows, at] * spread[rows, at]
                ys[rows, at] = exact_dot(stack3(decay), [head_blocks(part) for part in split3(x_dt)])
        for r in range(subs):
            rows = slice(r * SUB, (r + 1) * SUB)
            for n in range(n_piece):
                at = slice(n * PIECE, (n + 1) * PIECE)
                a_e = spread[CHUNK + r * SUB : CHUNK + (r + 1) * SUB, at]
                a_last = a_e[SUB - 1 : SUB]
                old = state[:, at]
                carried = exact_dot(c_stack[r], [part.astype(BF16) for part in split3(old)])
                x_act = xs[rows, at]
                ys[rows, at] = ys[rows, at] + carried * jnp.exp(a_e) + spread[2 * CHUNK : 2 * CHUNK + 1, at] * x_act
                tail_x = x_act * spread[rows, at] * jnp.exp(a_last - a_e)
                state[:, at] = jnp.exp(a_last) * old + exact_dot(bt_stack[r], [part.astype(BF16) for part in split3(tail_x)])

    def tail(layer, c, first):
        s = (layer * n_chunks + c) * subs
        gate_sq = jnp.zeros((CHUNK, 1), F32)
        if first:
            for cp in z_cp:
                cp.wait()
        for n in range(n_piece):
            at = slice(n * PIECE, (n + 1) * PIECE)
            z = dot(hbuf[...], wz[layer, n]).astype(BF16).astype(F32)
            v = ys[:, at] * jax.nn.silu(z)
            ys[:, at] = v
            gate_sq = gate_sq + jnp.sum(v * v, axis=1, keepdims=True)
        scale = scale_of(gate_sq)
        gbuf[...] = (ys[...] * scale * row_of(gw, layer)).astype(BF16)
        for r in range(subs):
            psend[s + r, 0, SUB:] = jnp.broadcast_to(to_row(gate_sq[r * SUB : (r + 1) * SUB]), (EXTRA, PIECE))
        if first:
            for cp in o_cp:
                cp.wait()
        for m in range(n_piece):
            part = dot(gbuf[...], wo[layer, 1 - core, m])
            for r in range(subs):
                psend[s + r, m, 0:SUB] = part[r * SUB : (r + 1) * SUB]
        if first:
            pl.semaphore_wait(barrier, 2)
        for r in range(subs):
            for m in range(n_piece):
                p_copy(s + r, m).start()
        for m in range(n_piece):
            part = dot(gbuf[...], wo[layer, core, m])
            for r in range(subs):
                own[r, m] = part[r * SUB : (r + 1) * SUB]

    def combine(s):
        for m in range(n_piece):
            p_copy(s, m).wait_recv()
            if m == 0:
                own_sq = to_col(psend[s, 0, SUB : SUB + 1])
                peer_sq = to_col(prcv[s, 0, SUB : SUB + 1])
                chip_sq = own_sq + peer_sq
                chip_scale = scale_of(chip_sq)
                f_own = chip_scale * inverse_of(own_sq)
                f_peer = chip_scale * inverse_of(peer_sq)
                qbuf[chip, s, 0, SUB:] = jnp.broadcast_to(to_row(chip_sq), (EXTRA, PIECE))
            qbuf[chip, s, m, 0:SUB] = own[s % subs, m] * f_own + prcv[s, m, 0:SUB] * f_peer
            q_copy(s, m).start()

    def update(s):
        layer, c = s // n_subs, s % n_subs
        for m in range(n_piece):
            q_copy(s, m).wait_recv()
            if m == 0:
                sq0 = to_col(qbuf[0, s, 0, SUB : SUB + 1])
                sq1 = to_col(qbuf[1, s, 0, SUB : SUB + 1])
                norm = lax.rsqrt((sq0 + sq1) / inner + EPSILON)
                f0 = norm * inverse_of(sq0)
                f1 = norm * inverse_of(sq1)
            total = ubuf[layer, core, c, m] + (qbuf[0, s, m, 0:SUB] * f0 + qbuf[1, s, m, 0:SUB] * f1)
            ubuf[layer + 1, core, c, m] = total.astype(BF16).astype(F32)
            u_copy(s, m).start()

    def emit(s):
        c = s % n_subs
        for side in (core, 1 - core):
            for m in range(n_piece):
                if side is not core:
                    u_copy(s, m).wait_recv()
                cols = pl.ds(pl.multiple_of(side * half + m * PIECE, PIECE), PIECE)
                out_ref[0, pl.ds(pl.multiple_of(c * SUB, SUB), SUB), cols] = ubuf[layers, side, c, m].astype(BF16)

    def load_hidden(c):
        hid_copy(c).wait()
        for side in range(2):
            for m in range(n_piece):
                at = side * half + m * PIECE
                ubuf[0, side, c, m] = hid[c, :, at : at + PIECE].astype(F32)

    start_layer()
    for r in range(subs):
        load_hidden(r)
    for cp in smalls:
        cp.wait()
    head(0, 0, True)
    tail(0, 0, True)
    later = [weight_copies(layer) for layer in range(1, layers)]
    for groups in later:
        groups[0].start()
        for group in groups[1:]:
            for cp in group:
                cp.start()
    for r in range(subs):
        combine(r)

    @pl.loop(1, layers * n_chunks)
    def _(t):
        layer, c = t // n_chunks, t % n_chunks
        for at in range(1, layers):
            @pl.when(t == at * n_chunks)
            def _():
                start_layer()
                later[at - 1][0].wait()
                for group in later[at - 1][1:]:
                    for cp in group:
                        cp.wait()

        @pl.when(t < n_chunks)
        def _():
            for r in range(subs):
                load_hidden(c * subs + r)

        @pl.when(t >= n_chunks)
        def _():
            before = (t - n_chunks) * subs
            for r in range(subs):
                update(before + r)
            for r in range(subs):
                for m in range(n_piece):
                    u_copy(before + r, m).wait_recv()

        head(layer, c, False)
        tail(layer, c, False)
        for r in range(subs):
            combine(t * subs + r)

    @pl.loop((layers - 1) * n_subs, layers * n_subs)
    def _(s):
        update(s)

    @pl.loop((layers - 1) * n_subs, layers * n_subs)
    def _(s):
        emit(s)

    @pl.loop(0, layers * n_subs)
    def _(s):
        for m in range(n_piece):
            p_copy(s, m).wait_send()
            q_copy(s, m).wait_send()
            u_copy(s, m).wait_send()


def solution(mesh):
    in_specs = (P('dp'), P(), P(None, None, 'tp'), P(None, None, 'tp'), P(), P(None, None, 'tp'), P(None, None, 'tp'), P(), P(None, 'tp'), P(),
                P(None, 'tp'), P(None, 'tp'), P(None, 'tp'), P(None, 'tp'), P(None, 'tp', None))
    tp_size = mesh.shape['tp']

    def device_forward(hidden, norm_w, w_z, w_x, w_bc, w_dt, conv_x, conv_bc, bias_x, bias_bc, dt_bias, a_log, d_skip, gate_w, w_out):
        layers, width, local = w_x.shape
        n_subs = hidden.shape[1] // SUB
        n_piece = local // PIECE
        steps = layers * n_subs
        bc_width = w_bc.shape[-1]
        w_dt = jnp.swapaxes(w_dt, 1, 2)
        vm = lambda shape, dtype: pltpu.VMEM(shape, dtype)
        same = lambda arr: pltpu.VMEM(arr.shape, arr.dtype)
        scratch = [
            vm((n_subs, SUB, width), BF16), same(norm_w), vm((layers, n_piece, width, PIECE), BF16), vm((layers, n_piece, width, PIECE), BF16),
            same(w_bc), same(w_dt), same(conv_x), same(conv_bc), same(bias_x), same(bias_bc), same(dt_bias), same(a_log), same(d_skip), same(gate_w),
            vm((layers, 2, n_piece, local, PIECE), BF16),
            vm((layers + 1, 2, n_subs, n_piece, SUB, PIECE), F32),
            vm((steps, n_piece, SUB + EXTRA, PIECE), F32), vm((steps, n_piece, SUB + EXTRA, PIECE), F32),
            vm((2, steps, n_piece, SUB + EXTRA, PIECE), F32),
            vm((CHUNK // SUB, n_piece, SUB, PIECE), F32), vm((CHUNK, width), BF16), vm((CHUNK + 8, local), F32), vm((CHUNK + 8, bc_width), F32),
            vm((CHUNK, local), F32), vm((CHUNK, local), F32), vm((2 * CHUNK + 8, local), F32), vm((HEAD, local), F32), vm((CHUNK, local), BF16),
            pltpu.SemaphoreType.DMA((10,)), pltpu.SemaphoreType.DMA((n_subs,)), pltpu.SemaphoreType.DMA((layers, 9 + 2 * n_piece)),
        ] + [pltpu.SemaphoreType.DMA((steps, n_piece)) for _ in range(6)]
        return pl.pallas_call(
            functools.partial(kernel, float(local * tp_size)),
            out_shape=jax.ShapeDtypeStruct(hidden.shape, hidden.dtype),
            in_specs=[pl.BlockSpec(memory_space=pltpu.HBM)] * 15,
            out_specs=pl.BlockSpec(memory_space=pltpu.VMEM),
            scratch_shapes=scratch,
            compiler_params=pltpu.CompilerParams(collective_id=0, has_side_effects=True, vmem_limit_bytes=52 * 1024 * 1024),
        )(*[pltpu.with_memory_space_constraint(arr, pltpu.HBM) for arr in (hidden, norm_w, w_z, w_x, w_bc, w_dt, conv_x, conv_bc, bias_x, bias_bc, dt_bias, a_log, d_skip, gate_w, w_out)])

    return jax.shard_map(device_forward, mesh=mesh, in_specs=in_specs, out_specs=P('dp'), check_vma=False)
```

time: 79.2 us -> 63.9 us (0.81)
  Pallas kernels: 76.8 us -> 62.8 us
  local copies, waits for them, and re-layouts: 2.3 us -> 0.97 us
    pallas_call x1, Pallas kernels: 76.8 us -> 62.8 us  [device_forward(): pl.pallas_call(functools.partial(kernel, float(local * tp_size)), out_sha...]
    unnamed x1, local copies, waits for them, and re-layouts: 2.3 us -> 0.97 us
where the time goes in v2:
time: 63.9 us; the launch traced here: 63.8 us
  Pallas kernels  62.8 us (98%)
  local copies, waits for them, and re-layouts  0.97 us (2%)
    pallas_call x1, Pallas kernels, device_forward(): pl.pallas_call(functools.partial(kernel, float(local * tp_size)), out_sha...  62.8 us

profile of v2, /device:TPU:0, one launch (start us, length us, event | category | flops | bytes accessed | tf_op | source)
XLA Modules:
  0.0 63.8 jit_solution(2349933628808543137)
XLA Ops:
  0.0 62.8 %shard_map.145 = bf16[1,256,2048]{2,1,0:T(8,128)(2,1)S(1)} custom-call(bf16[1,256,2048]{2,1,0:T(8,128)(2,1)} %hid_h.1, bf16[2,2048]{1,0:T(2,128)(2,1)} %nw_h.1, bf16[2,2048,1024]{2,1,0:T(8,128)(2,1)} %wz_h.1, bf16[2,2048,1024]{2,1,0:T(8,128)(2,1)} %wx_h.1, bf16[2,2048,128]{2,1,0:T(8,128)(2,1)} %wbc_h.1, bf16[2,16,2048]{2,1,0:T(8,128)(2,1)} %bitcast.1, ...), custom_call_target="tpu_custom_call" | custom-call | tf_op jit(solution)/shard_map/pallas_call | solution.py:410
  62.8 1.0 %copy.17 = bf16[1,256,2048]{2,1,0:T(8,128)(2,1)} copy(bf16[1,256,2048]{2,1,0:T(8,128)(2,1)S(1)} %shard_map.145) | data formatting | bytes 2097152

commit v3 on v2

v3 whole, which is shorter than its diff:
```python
import functools

import jax
import jax.numpy as jnp
from jax import lax
from jax.experimental import pallas as pl
from jax.experimental.pallas import tpu as pltpu
from jax.sharding import PartitionSpec as P

EPSILON = 1e-5
MESH = pl.DeviceIdType.MESH
SUB = 64
MAX_ROWS = 64
PIECE = 256
HEAD = 64
F32 = jnp.float32
BF16 = jnp.bfloat16


def split3(val):
    hi = val.astype(BF16).astype(F32)
    rest = val - hi
    mid = rest.astype(BF16).astype(F32)
    return hi, mid, rest - mid


def stack3(val):
    return jnp.concatenate(split3(val), axis=0).astype(BF16)


def dot(a, b):
    return lax.dot_general(a, b, (((1,), (0,)), ((), ())), preferred_element_type=F32)


def dot_nt(a, b):
    return lax.dot_general(a, b, (((1,), (1,)), ((), ())), preferred_element_type=F32)


def exact_dot(a_stack, b_parts, product=dot):
    rows = a_stack.shape[0] // 3
    b_hi, b_mid, b_lo = b_parts
    r1 = product(a_stack, b_hi)
    r2 = product(a_stack[: 2 * rows], b_mid)
    r3 = product(a_stack[:rows], b_lo)
    small = r1[2 * rows :] + r2[rows:] + r3
    return r1[:rows] + (r1[rows : 2 * rows] + r2[:rows] + small)


def iota(shape, dim):
    return lax.broadcasted_iota(jnp.int32, shape, dim)


def kernel(inner, hid_h, nw_h, wz_h, wx_h, wbc_h, wdt_h, cx_h, cbc_h, bx_h, bbc_h, dtb_h, al_h, ds_h, gw_h, wo_h,
           out_ref, hid, nw, wz, wx, wbc, wdt, cx, cbc, bx, bbc, dtb, al, ds, gw, wo,
           ubuf, psend, prcv, qbuf, pstat, qstat, own, hbuf, x0s, q0s, xs, ys, spread, state, gbuf,
           small_sem, hid_sem, w_sem, send_sem, pr_sem, qr_sem, ur_sem, ptr_sem, qtr_sem):
    me = lax.axis_index("tp")
    core = me % 2
    chip = me // 2
    peer = me + 1 - 2 * core
    cross = (me + 2) % 4
    n_subs = hid_h.shape[1] // SUB
    n_piece = wx_h.shape[2] // PIECE
    layers = nw_h.shape[0]
    local = wx_h.shape[2]
    half = wo_h.shape[2] // 2

    barrier = pltpu.get_barrier_semaphore()
    for other in (peer, cross):
        pl.semaphore_signal(barrier, inc=1, device_id={"tp": other}, device_id_type=MESH)

    smalls = [pltpu.make_async_copy(src, dst, small_sem.at[i]) for i, (src, dst) in enumerate(
        [(nw_h, nw), (cx_h, cx), (cbc_h, cbc), (bx_h, bx), (bbc_h, bbc), (dtb_h, dtb), (al_h, al), (ds_h, ds), (gw_h, gw), (wdt_h, wdt)])]

    def hid_copy(c):
        return pltpu.make_async_copy(hid_h.at[0, pl.ds(c * SUB, SUB)], hid.at[c], hid_sem.at[c])

    def weight_copies(layer):
        cols = lambda n: pl.ds(n * PIECE, PIECE)
        bc = pltpu.make_async_copy(wbc_h.at[layer], wbc.at[layer], w_sem.at[0])
        xcp = [pltpu.make_async_copy(wx_h.at[layer, :, cols(n)], wx.at[layer, n], w_sem.at[1 + n // 2]) for n in range(n_piece)]
        zcp = [pltpu.make_async_copy(wz_h.at[layer, :, cols(n)], wz.at[layer, n], w_sem.at[3]) for n in range(n_piece)]
        ocp = []
        for n in range(n_piece):
            for side in range(2):
                ocp.append(pltpu.make_async_copy(wo_h.at[layer, :, cols(side * n_piece + n)], wo.at[layer, side, n], w_sem.at[4]))
        return bc, xcp, zcp, ocp

    def weight_waits(layer):
        whole = lambda ref, sem: pltpu.make_async_copy(ref, ref, w_sem.at[sem])
        return [whole(wbc.at[layer], 0), whole(wx.at[layer, pl.ds(0, 2)], 1), whole(wx.at[layer, pl.ds(2, 2)], 2), whole(wz.at[layer], 3), whole(wo.at[layer], 4)]

    bc_cp, x_cp, z_cp, o_cp = weight_copies(0)
    first_wait = weight_waits(0)
    hid_copy(0).start()
    smalls[0].start()
    bc_cp.start()
    x_cp[0].start()
    x_cp[1].start()

    def remote(src, dst, sem, recv_sem, target):
        return pltpu.make_async_remote_copy(src_ref=src, dst_ref=dst, send_sem=send_sem.at[sem], recv_sem=recv_sem, device_id={"tp": target}, device_id_type=MESH)

    last = layers * n_subs - 1

    def own_slot(s, m):
        return s + m * (s // last)

    def p_copy(s, m):
        return remote(psend.at[s, m], prcv.at[s, m], 0, pr_sem.at[s % 2, m], peer)

    def pstat_copy(s):
        return remote(pstat.at[core, s], pstat.at[core, s], 1, ptr_sem.at[s % 2], peer)

    def q_copy(s, m):
        return remote(qbuf.at[chip, s, m], qbuf.at[chip, s, m], 2, qr_sem.at[own_slot(s, m)], cross)

    def qstat_copy(s):
        return remote(qstat.at[chip, s], qstat.at[chip, s], 3, qtr_sem.at[s], cross)

    def u_copy(s, m):
        spot = ubuf.at[s // n_subs + 1, core, s % n_subs, m]
        return remote(spot, spot, 4, ur_sem.at[own_slot(s, m)], peer)

    def q_arrived(s):
        remote(qbuf.at[chip, s], qbuf.at[chip, s], 2, qr_sem.at[s], cross).wait_recv()

    def u_arrived(s):
        spot = ubuf.at[s // n_subs + 1, core, s % n_subs]
        remote(spot, spot, 4, ur_sem.at[s], peer).wait_recv()

    def all_sent():
        shared = ubuf.at[pl.ds(1, layers), core]
        for sem, ref in enumerate((psend, pstat.at[core], qbuf.at[chip], qstat.at[chip], shared)):
            remote(ref, ref, sem, qtr_sem.at[0], cross).wait_send()

    row64 = iota((SUB, PIECE), 0)
    lane64 = iota((SUB, PIECE), 1) % HEAD
    eye = row64 == lane64
    causal = row64 >= lane64
    low_head = iota((SUB, 128), 1) < HEAD

    def to_row(col):
        return jnp.sum(jnp.where(eye, col, 0.0), axis=0, keepdims=True)

    def to_col(row):
        return jnp.sum(jnp.where(eye[:, :HEAD], row[:, :HEAD], 0.0), axis=1, keepdims=True)

    def scale_of(square_sum):
        return lax.rsqrt(square_sum / inner + EPSILON) * (1.0 / 64.0)

    def inverse_of(square_sum):
        return jnp.where(square_sum < jnp.inf, 64.0 * jnp.sqrt(square_sum / inner + EPSILON), 0.0)

    def head_blocks(part):
        left, right = part[:, :128], part[:, 128:]
        none = jnp.zeros_like(left)
        rows = [jnp.concatenate([jnp.where(low_head, left, 0.0), none], axis=1), jnp.concatenate([jnp.where(low_head, 0.0, left), none], axis=1),
                jnp.concatenate([none, jnp.where(low_head, right, 0.0)], axis=1), jnp.concatenate([none, jnp.where(low_head, 0.0, right)], axis=1)]
        return jnp.concatenate(rows, axis=0).astype(BF16)

    def row_of(ref, layer, lanes=slice(None)):
        row = ref[0:1, lanes]
        for at in range(1, layers):
            row = jnp.where(layer == at, ref[at : at + 1, lanes], row)
        return row.astype(F32)

    def start_layer():
        state[...] = jnp.zeros_like(state)
        x0s[0:8] = jnp.zeros((8, local), F32)
        q0s[0:8] = jnp.zeros((8, q0s.shape[1]), F32)

    def tap_sum(buf, size, lanes, kern, bias):
        total = bias
        for j in range(4):
            total = total + buf[5 + j : 5 + j + size, lanes] * kern[j : j + 1].astype(F32)
        return total

    def norm(layer, q, subs):
        square = [jnp.zeros((SUB, 1), F32) for _ in range(subs)]
        for r in range(subs):
            for side in range(2):
                for m in range(n_piece):
                    val = ubuf[layer, side, q + r, m]
                    square[r] = square[r] + jnp.sum(val * val, axis=1, keepdims=True)
        norm_row = row_of(nw, layer)
        for r in range(subs):
            scale = lax.rsqrt(square[r] / (2 * half) + EPSILON)
            for side in range(2):
                for m in range(n_piece):
                    at = side * half + m * PIECE
                    hbuf[r * SUB : (r + 1) * SUB, at : at + PIECE] = (ubuf[layer, side, q + r, m] * scale * norm_row[:, at : at + PIECE]).astype(BF16)

    def head(layer, q, subs, first, hook):
        size = subs * SUB
        if first:
            first_wait[0].wait()
            smalls[-1].wait()
        q0s[8 : 8 + size, :] = dot(hbuf[:size], wbc[layer]).astype(BF16).astype(F32)
        wdt3 = jnp.concatenate([wdt[layer]] * 3, axis=0)
        r_pre = dot_nt(hbuf[:size], wdt3).astype(BF16).astype(F32)
        for n in range(n_piece):
            at = slice(n * PIECE, (n + 1) * PIECE)
            if first and n % 2 == 0:
                first_wait[1 + n // 2].wait()
            x0s[8 : 8 + size, at] = dot(hbuf[:size], wx[layer, n]).astype(BF16).astype(F32)
        hook()
        if first:
            for cp in smalls[1:-1]:
                cp.wait()
            for cp in o_cp:
                cp.start()
        bc = jax.nn.silu(tap_sum(q0s, size, slice(None), cbc[layer], row_of(bbc, layer)))
        q0s[0:8] = q0s[size : size + 8]
        triple = lambda ref: jnp.concatenate([row_of(ref, layer)] * 3, axis=1)
        dt_in = r_pre + triple(dtb)
        dt_val = jnp.maximum(dt_in, 0.0) + jnp.log1p(jnp.exp(-jnp.abs(dt_in)))
        a_vals = -dt_val * jnp.exp(triple(al))
        to_t, from_t = iota((size, 3 * size), 0), iota((size, 3 * size), 1) % size
        tri = jnp.where((to_t >= from_t) & (to_t // SUB == from_t // SUB), 1.0, 0.0).astype(BF16)
        a_cum = dot(tri, stack3(a_vals))
        skip = jnp.broadcast_to(triple(ds), (8, a_cum.shape[1]))
        to_spread = jnp.concatenate([dt_val, a_cum, skip], axis=0)
        hi, mid, lo = split3(to_spread)
        lane = iota(to_spread.shape, 1)
        n_heads = local // HEAD
        spread_in = jnp.where(lane < n_heads, hi, jnp.where(lane < 2 * n_heads, mid, lo)).astype(BF16)
        for n in range(n_piece):
            at = slice(n * PIECE, (n + 1) * PIECE)
            group = n * (PIECE // HEAD)
            pick = jnp.where(iota((3 * n_heads, PIECE), 1) // HEAD + group == iota((3 * n_heads, PIECE), 0) % n_heads, 1.0, 0.0).astype(BF16)
            spread[: 2 * size + 8, at] = dot(spread_in, pick)
        swapped = pltpu.roll(bc, HEAD, 1)
        turned = jnp.transpose(bc)
        c_stack, bt_stack, cb = [], [], []
        for r in range(subs):
            rows = slice(r * SUB, (r + 1) * SUB)
            c_stack.append(stack3(swapped[rows, :HEAD]))
            bt_stack.append(stack3(turned[:HEAD, rows]))
            cb.append(exact_dot(c_stack[r], [jnp.concatenate([part] * 4, axis=0).astype(BF16) for part in split3(bc[rows, :HEAD])], dot_nt))
        for n in range(n_piece):
            at = slice(n * PIECE, (n + 1) * PIECE)
            xs[:size, at] = jax.nn.silu(tap_sum(x0s, size, at, cx[layer, :, at], row_of(bx, layer, at)))
            x0s[0:8, at] = x0s[size : size + 8, at]
        for r in range(subs):
            rows = slice(r * SUB, (r + 1) * SUB)
            for n in range(n_piece):
                at = slice(n * PIECE, (n + 1) * PIECE)
                a_e = spread[size + r * SUB : size + (r + 1) * SUB, at]
                decay = jnp.where(causal, jnp.exp(jnp.minimum(a_e - to_row(a_e), 0.0)), 0.0) * cb[r]
                x_dt = xs[rows, at] * spread[rows, at]
                ys[rows, at] = exact_dot(stack3(decay), [head_blocks(part) for part in split3(x_dt)])
        for r in range(subs):
            rows = slice(r * SUB, (r + 1) * SUB)
            for n in range(n_piece):
                at = slice(n * PIECE, (n + 1) * PIECE)
                a_e = spread[size + r * SUB : size + (r + 1) * SUB, at]
                a_last = a_e[SUB - 1 : SUB]
                old = state[:, at]
                carried = exact_dot(c_stack[r], [part.astype(BF16) for part in split3(old)])
                x_act = xs[rows, at]
                ys[rows, at] = ys[rows, at] + carried * jnp.exp(a_e) + spread[2 * size : 2 * size + 1, at] * x_act
                tail_x = x_act * spread[rows, at] * jnp.exp(a_last - a_e)
                state[:, at] = jnp.exp(a_last) * old + exact_dot(bt_stack[r], [part.astype(BF16) for part in split3(tail_x)])

    def tail(layer, q, subs, first):
        size = subs * SUB
        s = layer * n_subs + q
        gate_sq = jnp.zeros((size, 1), F32)
        if first:
            first_wait[3].wait()
        for n in range(n_piece):
            at = slice(n * PIECE, (n + 1) * PIECE)
            z = dot(hbuf[:size], wz[layer, n]).astype(BF16).astype(F32)
            v = ys[:size, at] * jax.nn.silu(z)
            ys[:size, at] = v
            gate_sq = gate_sq + jnp.sum(v * v, axis=1, keepdims=True)
        scale = scale_of(gate_sq)
        gbuf[:size] = (ys[:size] * scale * row_of(gw, layer)).astype(BF16)
        for r in range(subs):
            pstat[core, s + r] = to_row(gate_sq[r * SUB : (r + 1) * SUB])[:, :128]
        if first:
            for q_next in range(1, n_subs):
                hid_copy(q_next).start()
            first_wait[4].wait()
        for m in range(n_piece):
            part = dot(gbuf[:size], wo[layer, 1 - core, m])
            for r in range(subs):
                psend[s + r, m] = part[r * SUB : (r + 1) * SUB]
        if first:
            pl.semaphore_wait(barrier, 2)
        for r in range(subs):
            pstat_copy(s + r).start()
            for m in range(n_piece):
                p_copy(s + r, m).start()
        for m in range(n_piece):
            part = dot(gbuf[:size], wo[layer, core, m])
            for r in range(subs):
                own[m] = part[r * SUB : (r + 1) * SUB]

    def combine(s):
        pstat_copy(s).wait_recv()
        own_sq = to_col(pstat[core, s])
        peer_sq = to_col(pstat[1 - core, s])
        chip_sq = own_sq + peer_sq
        chip_scale = scale_of(chip_sq)
        f_own = chip_scale * inverse_of(own_sq)
        f_peer = chip_scale * inverse_of(peer_sq)
        qstat[chip, s] = to_row(chip_sq)[:, :128]
        qstat_copy(s).start()
        for m in range(n_piece):
            p_copy(s, m).wait_recv()
            qbuf[chip, s, m] = own[m] * f_own + prcv[s, m] * f_peer
            q_copy(s, m).start()

    def update(s, pieces=False):
        layer, c = s // n_subs, s % n_subs
        qstat_copy(s).wait_recv()
        if not pieces:
            q_arrived(s)
        sq0 = to_col(qstat[0, s])
        sq1 = to_col(qstat[1, s])
        norm = lax.rsqrt((sq0 + sq1) / inner + EPSILON)
        f0 = norm * inverse_of(sq0)
        f1 = norm * inverse_of(sq1)
        for m in range(n_piece):
            if pieces:
                q_copy(s, m).wait_recv()
            total = ubuf[layer, core, c, m] + (qbuf[0, s, m] * f0 + qbuf[1, s, m] * f1)
            ubuf[layer + 1, core, c, m] = total.astype(BF16).astype(F32)
            u_copy(s, m).start()

    def emit(s, pieces=False):
        c = s % n_subs
        for side in (core, 1 - core):
            if side is not core and not pieces:
                u_arrived(s)
            for m in range(n_piece):
                if side is not core and pieces:
                    u_copy(s, m).wait_recv()
                cols = pl.ds(pl.multiple_of(side * half + m * PIECE, PIECE), PIECE)
                out_ref[0, pl.ds(pl.multiple_of(c * SUB, SUB), SUB), cols] = ubuf[layers, side, c, m].astype(BF16)

    def load_hidden(c):
        hid_copy(c).wait()
        for side in range(2):
            for m in range(n_piece):
                at = side * half + m * PIECE
                ubuf[0, side, c, m] = hid[c, :, at : at + PIECE].astype(F32)

    steps = layers * n_subs
    lag = n_subs - 1
    steps = layers * n_subs
    lag = n_subs - 1
    start_layer()
    load_hidden(0)
    for cp in x_cp[2:] + smalls[-1:] + smalls[1:-1] + z_cp:
        cp.start()
    smalls[0].wait()
    norm(0, 0, 1)
    head(0, 0, 1, True, lambda: None)
    tail(0, 0, 1, True)

    def start_weights(layer):
        bc_cp, x_cp, z_cp, o_cp = weight_copies(layer)
        for cp in [bc_cp] + x_cp + z_cp + o_cp:
            cp.start()

    start_weights(1)
    combine(0)

    @pl.loop(1, steps)
    def _(t):
        layer, q = t // n_subs, t % n_subs

        @pl.when(t < n_subs)
        def _():
            load_hidden(q)

        @pl.when(t >= n_subs)
        def _():
            u_arrived(t - n_subs)

        for at in range(1, layers):
            @pl.when(t == at * n_subs)
            def _():
                start_layer()
                for cp in weight_waits(at):
                    cp.wait()
                if at + 1 < layers:
                    start_weights(at + 1)

        norm(layer, q, 1)

        @pl.when(t >= lag)
        def _():
            update(t - lag)

        def hook():
            @pl.when(t >= 2)
            def _():
                combine(t - 1)

        head(layer, q, 1, False, hook)
        tail(layer, q, 1, False)

    combine(steps - 1)
    final = steps - n_subs

    @pl.loop(final, steps - 1)
    def _(s):
        @pl.when(s > final)
        def _():
            emit(s - 1)

        @pl.when(s > steps - 1 - lag)
        def _():
            update(s)

    emit(steps - 2)
    update(steps - 1, True)
    emit(steps - 1, True)
    all_sent()


def solution(mesh):
    in_specs = (P('dp'), P(), P(None, None, 'tp'), P(None, None, 'tp'), P(), P(None, None, 'tp'), P(None, None, 'tp'), P(), P(None, 'tp'), P(),
                P(None, 'tp'), P(None, 'tp'), P(None, 'tp'), P(None, 'tp'), P(None, 'tp', None))
    tp_size = mesh.shape['tp']

    def device_forward(hidden, norm_w, w_z, w_x, w_bc, w_dt, conv_x, conv_bc, bias_x, bias_bc, dt_bias, a_log, d_skip, gate_w, w_out):
        layers, width, local = w_x.shape
        n_subs = hidden.shape[1] // SUB
        n_piece = local // PIECE
        steps = layers * n_subs
        bc_width = w_bc.shape[-1]
        w_dt = jnp.swapaxes(w_dt, 1, 2)
        vm = lambda shape, dtype: pltpu.VMEM(shape, dtype)
        same = lambda arr: pltpu.VMEM(arr.shape, arr.dtype)
        scratch = [
            vm((n_subs, SUB, width), BF16), same(norm_w), vm((layers, n_piece, width, PIECE), BF16), vm((layers, n_piece, width, PIECE), BF16),
            same(w_bc), same(w_dt), same(conv_x), same(conv_bc), same(bias_x), same(bias_bc), same(dt_bias), same(a_log), same(d_skip), same(gate_w),
            vm((layers, 2, n_piece, local, PIECE), BF16),
            vm((layers + 1, 2, n_subs, n_piece, SUB, PIECE), F32),
            vm((steps, n_piece, SUB, PIECE), F32), vm((steps, n_piece, SUB, PIECE), F32), vm((2, steps, n_piece, SUB, PIECE), F32),
            vm((2, steps, 1, 128), F32), vm((2, steps, 1, 128), F32),
            vm((n_piece, SUB, PIECE), F32), vm((MAX_ROWS, width), BF16), vm((MAX_ROWS + 8, local), F32), vm((MAX_ROWS + 8, bc_width), F32),
            vm((MAX_ROWS, local), F32), vm((MAX_ROWS, local), F32), vm((2 * MAX_ROWS + 8, local), F32), vm((HEAD, local), F32), vm((MAX_ROWS, local), BF16),
            pltpu.SemaphoreType.DMA((10,)), pltpu.SemaphoreType.DMA((n_subs,)), pltpu.SemaphoreType.DMA((5,)), pltpu.SemaphoreType.DMA((5,)),
            pltpu.SemaphoreType.DMA((2, n_piece)), pltpu.SemaphoreType.DMA((steps - 1 + n_piece,)), pltpu.SemaphoreType.DMA((steps - 1 + n_piece,)),
            pltpu.SemaphoreType.DMA((2,)), pltpu.SemaphoreType.DMA((steps,)),
        ]
        return pl.pallas_call(
            functools.partial(kernel, float(local * tp_size)),
            out_shape=jax.ShapeDtypeStruct(hidden.shape, hidden.dtype),
            in_specs=[pl.BlockSpec(memory_space=pltpu.HBM)] * 15,
            out_specs=pl.BlockSpec(memory_space=pltpu.VMEM),
            scratch_shapes=scratch,
            compiler_params=pltpu.CompilerParams(collective_id=0, has_side_effects=True, vmem_limit_bytes=52 * 1024 * 1024),
        )(*[pltpu.with_memory_space_constraint(arr, pltpu.HBM) for arr in (hidden, norm_w, w_z, w_x, w_bc, w_dt, conv_x, conv_bc, bias_x, bias_bc, dt_bias, a_log, d_skip, gate_w, w_out)])

    return jax.shard_map(device_forward, mesh=mesh, in_specs=in_specs, out_specs=P('dp'), check_vma=False)
```

time: 63.9 us -> 60.6 us (0.948)
  Pallas kernels: 62.8 us -> 59.5 us
    pallas_call x1, Pallas kernels: 62.8 us -> 59.5 us  [device_forward(): pl.pallas_call(functools.partial(kernel, float(local * tp_size)), out_sha...]
where the time goes in v3:
time: 60.6 us; the launch traced here: 60.5 us
  Pallas kernels  59.5 us (98%)
  local copies, waits for them, and re-layouts  0.97 us (2%)
    pallas_call x1, Pallas kernels, device_forward(): pl.pallas_call(functools.partial(kernel, float(local * tp_size)), out_sha...  59.5 us

profile of v3, /device:TPU:0, one launch (start us, length us, event | category | flops | bytes accessed | tf_op | source)
XLA Modules:
  0.0 60.5 jit_solution(13143679731067620498)
XLA Ops:
  0.0 59.5 %shard_map.145 = bf16[1,256,2048]{2,1,0:T(8,128)(2,1)S(1)} custom-call(bf16[1,256,2048]{2,1,0:T(8,128)(2,1)} %hid_h.1, bf16[2,2048]{1,0:T(2,128)(2,1)} %nw_h.1, bf16[2,2048,1024]{2,1,0:T(8,128)(2,1)} %wz_h.1, bf16[2,2048,1024]{2,1,0:T(8,128)(2,1)} %wx_h.1, bf16[2,2048,128]{2,1,0:T(8,128)(2,1)} %wbc_h.1, bf16[2,16,2048]{2,1,0:T(8,128)(2,1)} %bitcast.1, ...), custom_call_target="tpu_custom_call" | custom-call | tf_op jit(solution)/shard_map/pallas_call | solution.py:453
  59.5 1.0 %copy.17 = bf16[1,256,2048]{2,1,0:T(8,128)(2,1)} copy(bf16[1,256,2048]{2,1,0:T(8,128)(2,1)S(1)} %shard_map.145) | data formatting | bytes 2097152

commit v4 on v3

--- a/solution.py
+++ b/solution.py
@@ -51,8 +51,8 @@
 
 
 def kernel(inner, hid_h, nw_h, wz_h, wx_h, wbc_h, wdt_h, cx_h, cbc_h, bx_h, bbc_h, dtb_h, al_h, ds_h, gw_h, wo_h,
-           out_ref, hid, nw, wz, wx, wbc, wdt, cx, cbc, bx, bbc, dtb, al, ds, gw, wo,
-           ubuf, psend, prcv, qbuf, pstat, qstat, own, hbuf, x0s, q0s, xs, ys, spread, state, gbuf,
+           out_ref, hid, nw, wz, wx, wbd, wdt, cx, cbc, bx, bbc, dtb, al, ds, gw, wo,
+           ubuf, psend, prcv, qbuf, pstat, qstat, own, hbuf, x0s, q0s, xs, ys, zs, spread, state, gbuf,
            small_sem, hid_sem, w_sem, send_sem, pr_sem, qr_sem, ur_sem, ptr_sem, qtr_sem):
     me = lax.axis_index("tp")
     core = me % 2
@@ -75,28 +75,37 @@
     def hid_copy(c):
         return pltpu.make_async_copy(hid_h.at[0, pl.ds(c * SUB, SUB)], hid.at[c], hid_sem.at[c])
 
-    def weight_copies(layer):
-        cols = lambda n: pl.ds(n * PIECE, PIECE)
-        bc = pltpu.make_async_copy(wbc_h.at[layer], wbc.at[layer], w_sem.at[0])
-        xcp = [pltpu.make_async_copy(wx_h.at[layer, :, cols(n)], wx.at[layer, n], w_sem.at[1 + n // 2]) for n in range(n_piece)]
-        zcp = [pltpu.make_async_copy(wz_h.at[layer, :, cols(n)], wz.at[layer, n], w_sem.at[3]) for n in range(n_piece)]
-        ocp = []
-        for n in range(n_piece):
-            for side in range(2):
-                ocp.append(pltpu.make_async_copy(wo_h.at[layer, :, cols(side * n_piece + n)], wo.at[layer, side, n], w_sem.at[4]))
-        return bc, xcp, zcp, ocp
+    def start_weights(layer, extra=()):
+        cols = lambda n: pl.ds(pl.multiple_of(n * PIECE, PIECE), PIECE)
+
+        @pl.loop(0, n_piece)
+        def _(n):
+            pltpu.make_async_copy(wx_h.at[layer, :, cols(n)], wx.at[layer, n], w_sem.at[1 + n // 2]).start()
+
+        for cp in extra:
+            cp.start()
+
+        @pl.loop(0, n_piece)
+        def _(n):
+            pltpu.make_async_copy(wz_h.at[layer, :, cols(n)], wz.at[layer, n], w_sem.at[3]).start()
+
+        @pl.loop(0, 2 * n_piece)
+        def _(n):
+            pltpu.make_async_copy(wo_h.at[layer, :, cols(n)], wo.at[layer, n // n_piece, n % n_piece], w_sem.at[4]).start()
+
+    def bc_copy(layer):
+        return pltpu.make_async_copy(wbc_h.at[layer], wbd.at[layer, :, pl.ds(0, 2 * HEAD)], w_sem.at[0])
 
     def weight_waits(layer):
         whole = lambda ref, sem: pltpu.make_async_copy(ref, ref, w_sem.at[sem])
-        return [whole(wbc.at[layer], 0), whole(wx.at[layer, pl.ds(0, 2)], 1), whole(wx.at[layer, pl.ds(2, 2)], 2), whole(wz.at[layer], 3), whole(wo.at[layer], 4)]
-
-    bc_cp, x_cp, z_cp, o_cp = weight_copies(0)
+        return [whole(wbd.at[layer, :, pl.ds(0, 2 * HEAD)], 0), whole(wx.at[layer, pl.ds(0, 2)], 1), whole(wx.at[layer, pl.ds(2, 2)], 2), whole(wz.at[layer], 3), whole(wo.at[layer], 4)]
+
     first_wait = weight_waits(0)
-    hid_copy(0).start()
-    smalls[0].start()
-    bc_cp.start()
-    x_cp[0].start()
-    x_cp[1].start()
+    for cp in [smalls[0], smalls[-1], hid_copy(0), bc_copy(0)]:
+        cp.start()
+    start_weights(0, smalls[1:-1])
+    for q in range(1, n_subs):
+        hid_copy(q).start()
 
     def remote(src, dst, sem, recv_sem, target):
         return pltpu.make_async_remote_copy(src_ref=src, dst_ref=dst, send_sem=send_sem.at[sem], recv_sem=recv_sem, device_id={"tp": target}, device_id_type=MESH)
@@ -165,6 +174,12 @@
             row = jnp.where(layer == at, ref[at : at + 1, lanes], row)
         return row.astype(F32)
 
+    def turn_wdt(layer):
+        for k in range(0, wdt.shape[2], 128):
+            block = wdt[layer, :, k : k + 128].astype(F32)
+            turned = jnp.transpose(jnp.concatenate([block] * 3, axis=0)).astype(BF16)
+            wbd[layer, k : k + 128, 2 * HEAD : 2 * HEAD + turned.shape[1]] = turned
+
     def start_layer():
         state[...] = jnp.zeros_like(state)
         x0s[0:8] = jnp.zeros((8, local), F32)
@@ -195,21 +210,19 @@
         size = subs * SUB
         if first:
             first_wait[0].wait()
-            smalls[-1].wait()
-        q0s[8 : 8 + size, :] = dot(hbuf[:size], wbc[layer]).astype(BF16).astype(F32)
-        wdt3 = jnp.concatenate([wdt[layer]] * 3, axis=0)
-        r_pre = dot_nt(hbuf[:size], wdt3).astype(BF16).astype(F32)
+        both = dot(hbuf[:size], wbd[layer]).astype(BF16).astype(F32)
+        q0s[8 : 8 + size, :] = both[:, : 2 * HEAD]
+        r_pre = both[:, 2 * HEAD : 2 * HEAD + 3 * (local // HEAD)]
         for n in range(n_piece):
             at = slice(n * PIECE, (n + 1) * PIECE)
             if first and n % 2 == 0:
                 first_wait[1 + n // 2].wait()
             x0s[8 : 8 + size, at] = dot(hbuf[:size], wx[layer, n]).astype(BF16).astype(F32)
-        hook()
+            if n == 1:
+                hook()
         if first:
             for cp in smalls[1:-1]:
                 cp.wait()
-            for cp in o_cp:
-                cp.start()
         bc = jax.nn.silu(tap_sum(q0s, size, slice(None), cbc[layer], row_of(bbc, layer)))
         q0s[0:8] = q0s[size : size + 8]
         triple = lambda ref: jnp.concatenate([row_of(ref, layer)] * 3, axis=1)
@@ -242,6 +255,11 @@
             at = slice(n * PIECE, (n + 1) * PIECE)
             xs[:size, at] = jax.nn.silu(tap_sum(x0s, size, at, cx[layer, :, at], row_of(bx, layer, at)))
             x0s[0:8, at] = x0s[size : size + 8, at]
+        if first:
+            first_wait[3].wait()
+        for n in range(n_piece):
+            at = slice(n * PIECE, (n + 1) * PIECE)
+            zs[:size, at] = jax.nn.silu(dot(hbuf[:size], wz[layer, n]).astype(BF16).astype(F32))
         for r in range(subs):
             rows = slice(r * SUB, (r + 1) * SUB)
             for n in range(n_piece):
@@ -267,12 +285,9 @@
         size = subs * SUB
         s = layer * n_subs + q
         gate_sq = jnp.zeros((size, 1), F32)
-        if first:
-            first_wait[3].wait()
         for n in range(n_piece):
             at = slice(n * PIECE, (n + 1) * PIECE)
-            z = dot(hbuf[:size], wz[layer, n]).astype(BF16).astype(F32)
-            v = ys[:size, at] * jax.nn.silu(z)
+            v = ys[:size, at] * zs[:size, at]
             ys[:size, at] = v
             gate_sq = gate_sq + jnp.sum(v * v, axis=1, keepdims=True)
         scale = scale_of(gate_sq)
@@ -280,8 +295,6 @@
         for r in range(subs):
             pstat[core, s + r] = to_row(gate_sq[r * SUB : (r + 1) * SUB])[:, :128]
         if first:
-            for q_next in range(1, n_subs):
-                hid_copy(q_next).start()
             first_wait[4].wait()
         for m in range(n_piece):
             part = dot(gbuf[:size], wo[layer, 1 - core, m])
@@ -353,19 +366,15 @@
     steps = layers * n_subs
     lag = n_subs - 1
     start_layer()
+    smalls[0].wait()
     load_hidden(0)
-    for cp in x_cp[2:] + smalls[-1:] + smalls[1:-1] + z_cp:
-        cp.start()
-    smalls[0].wait()
     norm(0, 0, 1)
+    smalls[-1].wait()
+    turn_wdt(0)
     head(0, 0, 1, True, lambda: None)
     tail(0, 0, 1, True)
 
-    def start_weights(layer):
-        bc_cp, x_cp, z_cp, o_cp = weight_copies(layer)
-        for cp in [bc_cp] + x_cp + z_cp + o_cp:
-            cp.start()
-
+    bc_copy(1).start()
     start_weights(1)
     combine(0)
 
@@ -385,9 +394,11 @@
             @pl.when(t == at * n_subs)
             def _():
                 start_layer()
+                turn_wdt(at)
                 for cp in weight_waits(at):
                     cp.wait()
                 if at + 1 < layers:
+                    bc_copy(at + 1).start()
                     start_weights(at + 1)
 
         norm(layer, q, 1)
@@ -439,13 +450,13 @@
         same = lambda arr: pltpu.VMEM(arr.shape, arr.dtype)
         scratch = [
             vm((n_subs, SUB, width), BF16), same(norm_w), vm((layers, n_piece, width, PIECE), BF16), vm((layers, n_piece, width, PIECE), BF16),
-            same(w_bc), same(w_dt), same(conv_x), same(conv_bc), same(bias_x), same(bias_bc), same(dt_bias), same(a_log), same(d_skip), same(gate_w),
+            vm((layers, width, PIECE), BF16), same(w_dt), same(conv_x), same(conv_bc), same(bias_x), same(bias_bc), same(dt_bias), same(a_log), same(d_skip), same(gate_w),
             vm((layers, 2, n_piece, local, PIECE), BF16),
             vm((layers + 1, 2, n_subs, n_piece, SUB, PIECE), F32),
             vm((steps, n_piece, SUB, PIECE), F32), vm((steps, n_piece, SUB, PIECE), F32), vm((2, steps, n_piece, SUB, PIECE), F32),
             vm((2, steps, 1, 128), F32), vm((2, steps, 1, 128), F32),
             vm((n_piece, SUB, PIECE), F32), vm((MAX_ROWS, width), BF16), vm((MAX_ROWS + 8, local), F32), vm((MAX_ROWS + 8, bc_width), F32),
-            vm((MAX_ROWS, local), F32), vm((MAX_ROWS, local), F32), vm((2 * MAX_ROWS + 8, local), F32), vm((HEAD, local), F32), vm((MAX_ROWS, local), BF16),
+            vm((MAX_ROWS, local), F32), vm((MAX_ROWS, local), F32), vm((MAX_ROWS, local), F32), vm((2 * MAX_ROWS + 8, local), F32), vm((HEAD, local), F32), vm((MAX_ROWS, local), BF16),
             pltpu.SemaphoreType.DMA((10,)), pltpu.SemaphoreType.DMA((n_subs,)), pltpu.SemaphoreType.DMA((5,)), pltpu.SemaphoreType.DMA((5,)),
             pltpu.SemaphoreType.DMA((2, n_piece)), pltpu.SemaphoreType.DMA((steps - 1 + n_piece,)), pltpu.SemaphoreType.DMA((steps - 1 + n_piece,)),
             pltpu.SemaphoreType.DMA((2,)), pltpu.SemaphoreType.DMA((steps,)),

time: 60.6 us -> 59.3 us (0.979)
  Pallas kernels: 59.5 us -> 58.1 us
    pallas_call x1, Pallas kernels: 59.5 us -> 58.1 us  [device_forward(): pl.pallas_call(functools.partial(kernel, float(local * tp_size)), out_sha...]
where the time goes in v4:
time: 59.3 us; the launch traced here: 59.1 us
  Pallas kernels  58.1 us (98%)
  local copies, waits for them, and re-layouts  0.97 us (2%)
    pallas_call x1, Pallas kernels, device_forward(): pl.pallas_call(functools.partial(kernel, float(local * tp_size)), out_sha...  58.1 us

profile of v4, /device:TPU:0, one launch (start us, length us, event | category | flops | bytes accessed | tf_op | source)
XLA Modules:
  0.0 59.1 jit_solution(7305019885645223390)
XLA Ops:
  0.0 58.1 %shard_map.145 = bf16[1,256,2048]{2,1,0:T(8,128)(2,1)S(1)} custom-call(bf16[1,256,2048]{2,1,0:T(8,128)(2,1)} %hid_h.1, bf16[2,2048]{1,0:T(2,128)(2,1)} %nw_h.1, bf16[2,2048,1024]{2,1,0:T(8,128)(2,1)} %wz_h.1, bf16[2,2048,1024]{2,1,0:T(8,128)(2,1)} %wx_h.1, bf16[2,2048,128]{2,1,0:T(8,128)(2,1)} %wbc_h.1, bf16[2,16,2048]{2,1,0:T(8,128)(2,1)} %bitcast.1, ...), custom_call_target="tpu_custom_call" | custom-call | tf_op jit(solution)/shard_map/pallas_call | solution.py:464
  58.1 1.0 %copy.17 = bf16[1,256,2048]{2,1,0:T(8,128)(2,1)} copy(bf16[1,256,2048]{2,1,0:T(8,128)(2,1)S(1)} %shard_map.145) | data formatting | bytes 2097152

commit v5 on v4

--- a/solution.py
+++ b/solution.py
@@ -11,6 +11,8 @@
 MESH = pl.DeviceIdType.MESH
 SUB = 64
 MAX_ROWS = 64
+ORDER_FIRST = "x2 i0 x3 i1 c2 a0 c3 a1 i2 a2 i3 a3 wait z0 z1 z2 z3"
+ORDER_LATER = "c0 z0 c1 i0 c2 z1 i1 a0 c3 z2 i2 a1 z3 i3 a2 a3"
 PIECE = 256
 HEAD = 64
 F32 = jnp.float32
@@ -52,7 +54,7 @@
 
 def kernel(inner, hid_h, nw_h, wz_h, wx_h, wbc_h, wdt_h, cx_h, cbc_h, bx_h, bbc_h, dtb_h, al_h, ds_h, gw_h, wo_h,
            out_ref, hid, nw, wz, wx, wbd, wdt, cx, cbc, bx, bbc, dtb, al, ds, gw, wo,
-           ubuf, psend, prcv, qbuf, pstat, qstat, own, hbuf, x0s, q0s, xs, ys, zs, spread, state, gbuf,
+           ubuf, psend, prcv, qbuf, pstat, qstat, own, hbuf, x0s, q0s, xs, ys, zs, dstack, spread, state, gbuf,
            small_sem, hid_sem, w_sem, send_sem, pr_sem, qr_sem, ur_sem, ptr_sem, qtr_sem):
     me = lax.axis_index("tp")
     core = me % 2
@@ -75,35 +77,33 @@
     def hid_copy(c):
         return pltpu.make_async_copy(hid_h.at[0, pl.ds(c * SUB, SUB)], hid.at[c], hid_sem.at[c])
 
-    def start_weights(layer, extra=()):
+    def start_weights(layer):
         cols = lambda n: pl.ds(pl.multiple_of(n * PIECE, PIECE), PIECE)
 
         @pl.loop(0, n_piece)
         def _(n):
             pltpu.make_async_copy(wx_h.at[layer, :, cols(n)], wx.at[layer, n], w_sem.at[1 + n // 2]).start()
 
-        for cp in extra:
-            cp.start()
-
         @pl.loop(0, n_piece)
         def _(n):
             pltpu.make_async_copy(wz_h.at[layer, :, cols(n)], wz.at[layer, n], w_sem.at[3]).start()
 
         @pl.loop(0, 2 * n_piece)
         def _(n):
-            pltpu.make_async_copy(wo_h.at[layer, :, cols(n)], wo.at[layer, n // n_piece, n % n_piece], w_sem.at[4]).start()
+            side = (n // n_piece + 1 - core) % 2
+            pltpu.make_async_copy(wo_h.at[layer, :, cols(side * n_piece + n % n_piece)], wo.at[layer, side, n % n_piece], w_sem.at[4 + n // n_piece]).start()
 
     def bc_copy(layer):
         return pltpu.make_async_copy(wbc_h.at[layer], wbd.at[layer, :, pl.ds(0, 2 * HEAD)], w_sem.at[0])
 
     def weight_waits(layer):
         whole = lambda ref, sem: pltpu.make_async_copy(ref, ref, w_sem.at[sem])
-        return [whole(wbd.at[layer, :, pl.ds(0, 2 * HEAD)], 0), whole(wx.at[layer, pl.ds(0, 2)], 1), whole(wx.at[layer, pl.ds(2, 2)], 2), whole(wz.at[layer], 3), whole(wo.at[layer], 4)]
+        return [whole(wbd.at[layer, :, pl.ds(0, 2 * HEAD)], 0), whole(wx.at[layer, pl.ds(0, 2)], 1), whole(wx.at[layer, pl.ds(2, 2)], 2), whole(wz.at[layer], 3), whole(wo.at[layer, 1 - core], 4), whole(wo.at[layer, core], 5)]
 
     first_wait = weight_waits(0)
-    for cp in [smalls[0], smalls[-1], hid_copy(0), bc_copy(0)]:
+    for cp in [smalls[0], smalls[-1], hid_copy(0), bc_copy(0)] + smalls[1:-1]:
         cp.start()
-    start_weights(0, smalls[1:-1])
+    start_weights(0)
     for q in range(1, n_subs):
         hid_copy(q).start()
 
@@ -206,6 +206,12 @@
                     at = side * half + m * PIECE
                     hbuf[r * SUB : (r + 1) * SUB, at : at + PIECE] = (ubuf[layer, side, q + r, m] * scale * norm_row[:, at : at + PIECE]).astype(BF16)
 
+    def x_product(layer, size, n):
+        x0s[8 : 8 + size, n * PIECE : (n + 1) * PIECE] = dot(hbuf[:size], wx[layer, n]).astype(BF16).astype(F32)
+
+    def z_product(layer, size, n):
+        zs[:size, n * PIECE : (n + 1) * PIECE] = jax.nn.silu(dot(hbuf[:size], wz[layer, n]).astype(BF16).astype(F32))
+
     def head(layer, q, subs, first, hook):
         size = subs * SUB
         if first:
@@ -213,16 +219,15 @@
         both = dot(hbuf[:size], wbd[layer]).astype(BF16).astype(F32)
         q0s[8 : 8 + size, :] = both[:, : 2 * HEAD]
         r_pre = both[:, 2 * HEAD : 2 * HEAD + 3 * (local // HEAD)]
-        for n in range(n_piece):
-            at = slice(n * PIECE, (n + 1) * PIECE)
-            if first and n % 2 == 0:
-                first_wait[1 + n // 2].wait()
-            x0s[8 : 8 + size, at] = dot(hbuf[:size], wx[layer, n]).astype(BF16).astype(F32)
-            if n == 1:
-                hook()
         if first:
             for cp in smalls[1:-1]:
                 cp.wait()
+        if not first:
+            x_product(layer, size, 0)
+            x_product(layer, size, 1)
+            hook()
+            x_product(layer, size, 2)
+            x_product(layer, size, 3)
         bc = jax.nn.silu(tap_sum(q0s, size, slice(None), cbc[layer], row_of(bbc, layer)))
         q0s[0:8] = q0s[size : size + 8]
         triple = lambda ref: jnp.concatenate([row_of(ref, layer)] * 3, axis=1)
@@ -251,27 +256,29 @@
             c_stack.append(stack3(swapped[rows, :HEAD]))
             bt_stack.append(stack3(turned[:HEAD, rows]))
             cb.append(exact_dot(c_stack[r], [jnp.concatenate([part] * 4, axis=0).astype(BF16) for part in split3(bc[rows, :HEAD])], dot_nt))
-        for n in range(n_piece):
+        for r in range(subs):
+            rows = slice(3 * r * SUB, 3 * (r + 1) * SUB)
+            for n in range(n_piece):
+                at = slice(n * PIECE, (n + 1) * PIECE)
+                a_e = spread[size + r * SUB : size + (r + 1) * SUB, at]
+                dstack[rows, at] = stack3(jnp.where(causal, jnp.exp(jnp.minimum(a_e - to_row(a_e), 0.0)), 0.0) * cb[r])
+
+        def conv(n):
             at = slice(n * PIECE, (n + 1) * PIECE)
             xs[:size, at] = jax.nn.silu(tap_sum(x0s, size, at, cx[layer, :, at], row_of(bx, layer, at)))
             x0s[0:8, at] = x0s[size : size + 8, at]
-        if first:
-            first_wait[3].wait()
-        for n in range(n_piece):
+
+        def inside(n):
             at = slice(n * PIECE, (n + 1) * PIECE)
-            zs[:size, at] = jax.nn.silu(dot(hbuf[:size], wz[layer, n]).astype(BF16).astype(F32))
-        for r in range(subs):
-            rows = slice(r * SUB, (r + 1) * SUB)
-            for n in range(n_piece):
-                at = slice(n * PIECE, (n + 1) * PIECE)
-                a_e = spread[size + r * SUB : size + (r + 1) * SUB, at]
-                decay = jnp.where(causal, jnp.exp(jnp.minimum(a_e - to_row(a_e), 0.0)), 0.0) * cb[r]
+            for r in range(subs):
+                rows = slice(r * SUB, (r + 1) * SUB)
                 x_dt = xs[rows, at] * spread[rows, at]
-                ys[rows, at] = exact_dot(stack3(decay), [head_blocks(part) for part in split3(x_dt)])
-        for r in range(subs):
-            rows = slice(r * SUB, (r + 1) * SUB)
-            for n in range(n_piece):
-                at = slice(n * PIECE, (n + 1) * PIECE)
+                ys[rows, at] = exact_dot(dstack[3 * r * SUB : 3 * (r + 1) * SUB, at], [head_blocks(part) for part in split3(x_dt)])
+
+        def across(n):
+            at = slice(n * PIECE, (n + 1) * PIECE)
+            for r in range(subs):
+                rows = slice(r * SUB, (r + 1) * SUB)
                 a_e = spread[size + r * SUB : size + (r + 1) * SUB, at]
                 a_last = a_e[SUB - 1 : SUB]
                 old = state[:, at]
@@ -280,6 +287,21 @@
                 ys[rows, at] = ys[rows, at] + carried * jnp.exp(a_e) + spread[2 * size : 2 * size + 1, at] * x_act
                 tail_x = x_act * spread[rows, at] * jnp.exp(a_last - a_e)
                 state[:, at] = jnp.exp(a_last) * old + exact_dot(bt_stack[r], [part.astype(BF16) for part in split3(tail_x)])
+
+        if first:
+            first_wait[1].wait()
+            x_product(layer, size, 0)
+            x_product(layer, size, 1)
+            conv(0)
+            conv(1)
+            first_wait[2].wait()
+        plan = ORDER_FIRST if first else ORDER_LATER
+        stages = {"x": lambda n: x_product(layer, size, n), "c": conv, "i": inside, "a": across, "z": lambda n: z_product(layer, size, n)}
+        for step in plan.split():
+            if step == "wait":
+                first_wait[3].wait()
+            else:
+                stages[step[0]](int(step[1]))
 
     def tail(layer, q, subs, first):
         size = subs * SUB
@@ -306,6 +328,8 @@
             pstat_copy(s + r).start()
             for m in range(n_piece):
                 p_copy(s + r, m).start()
+        if first:
+            first_wait[5].wait()
         for m in range(n_piece):
             part = dot(gbuf[:size], wo[layer, core, m])
             for r in range(subs):
@@ -367,10 +391,10 @@
     lag = n_subs - 1
     start_layer()
     smalls[0].wait()
+    smalls[-1].wait()
+    turn_wdt(0)
     load_hidden(0)
     norm(0, 0, 1)
-    smalls[-1].wait()
-    turn_wdt(0)
     head(0, 0, 1, True, lambda: None)
     tail(0, 0, 1, True)
 
@@ -403,12 +427,16 @@
 
         norm(layer, q, 1)
 
+        @pl.when(t == 2)
+        def _():
+            combine(t - 1)
+
         @pl.when(t >= lag)
         def _():
             update(t - lag)
 
         def hook():
-            @pl.when(t >= 2)
+            @pl.when(t > 2)
             def _():
                 combine(t - 1)
 
@@ -456,8 +484,8 @@
             vm((steps, n_piece, SUB, PIECE), F32), vm((steps, n_piece, SUB, PIECE), F32), vm((2, steps, n_piece, SUB, PIECE), F32),
             vm((2, steps, 1, 128), F32), vm((2, steps, 1, 128), F32),
             vm((n_piece, SUB, PIECE), F32), vm((MAX_ROWS, width), BF16), vm((MAX_ROWS + 8, local), F32), vm((MAX_ROWS + 8, bc_width), F32),
-            vm((MAX_ROWS, local), F32), vm((MAX_ROWS, local), F32), vm((MAX_ROWS, local), F32), vm((2 * MAX_ROWS + 8, local), F32), vm((HEAD, local), F32), vm((MAX_ROWS, local), BF16),
-            pltpu.SemaphoreType.DMA((10,)), pltpu.SemaphoreType.DMA((n_subs,)), pltpu.SemaphoreType.DMA((5,)), pltpu.SemaphoreType.DMA((5,)),
+            vm((MAX_ROWS, local), F32), vm((MAX_ROWS, local), F32), vm((MAX_ROWS, local), F32), vm((3 * MAX_ROWS, local), BF16), vm((2 * MAX_ROWS + 8, local), F32), vm((HEAD, local), F32), vm((MAX_ROWS, local), BF16),
+            pltpu.SemaphoreType.DMA((10,)), pltpu.SemaphoreType.DMA((n_subs,)), pltpu.SemaphoreType.DMA((6,)), pltpu.SemaphoreType.DMA((5,)),
             pltpu.SemaphoreType.DMA((2, n_piece)), pltpu.SemaphoreType.DMA((steps - 1 + n_piece,)), pltpu.SemaphoreType.DMA((steps - 1 + n_piece,)),
             pltpu.SemaphoreType.DMA((2,)), pltpu.SemaphoreType.DMA((steps,)),
         ]

time: 59.3 us -> 58.8 us (level)
  no operation moved by 1% of the time
where the time goes in v5:
time: 58.8 us; the launch traced here: 58.7 us
  Pallas kernels  57.7 us (98%)
  local copies, waits for them, and re-layouts  0.97 us (2%)
    pallas_call x1, Pallas kernels, device_forward(): pl.pallas_call(functools.partial(kernel, float(local * tp_size)), out_sha...  57.7 us

profile of v5, /device:TPU:0, one launch (start us, length us, event | category | flops | bytes accessed | tf_op | source)
XLA Modules:
  0.0 58.7 jit_solution(11674558762214283513)
XLA Ops:
  0.0 57.7 %shard_map.145 = bf16[1,256,2048]{2,1,0:T(8,128)(2,1)S(1)} custom-call(bf16[1,256,2048]{2,1,0:T(8,128)(2,1)} %hid_h.1, bf16[2,2048]{1,0:T(2,128)(2,1)} %nw_h.1, bf16[2,2048,1024]{2,1,0:T(8,128)(2,1)} %wz_h.1, bf16[2,2048,1024]{2,1,0:T(8,128)(2,1)} %wx_h.1, bf16[2,2048,128]{2,1,0:T(8,128)(2,1)} %wbc_h.1, bf16[2,16,2048]{2,1,0:T(8,128)(2,1)} %bitcast.1, ...), custom_call_target="tpu_custom_call" | custom-call | tf_op jit(solution)/shard_map/pallas_call | solution.py:492
  57.7 1.0 %copy.17 = bf16[1,256,2048]{2,1,0:T(8,128)(2,1)} copy(bf16[1,256,2048]{2,1,0:T(8,128)(2,1)S(1)} %shard_map.145) | data formatting | bytes 2097152

commit v6 on v5

--- a/solution.py
+++ b/solution.py
@@ -11,8 +11,8 @@
 MESH = pl.DeviceIdType.MESH
 SUB = 64
 MAX_ROWS = 64
-ORDER_FIRST = "x2 i0 x3 i1 c2 a0 c3 a1 i2 a2 i3 a3 wait z0 z1 z2 z3"
-ORDER_LATER = "c0 z0 c1 i0 c2 z1 i1 a0 c3 z2 i2 a1 z3 i3 a2 a3"
+ORDER_FIRST = ("x2", "i0", "x3", "i1", "c2", "a0", "c3", "a1", "i2", "a2", "i3", "a3", "wait", "z0", "z1", "z2", "z3")
+ORDER_LATER = ("c0", "z0", "c1", "i0", "c2", "z1", "i1", "a0", "c3", "z2", "i2", "a1", "z3", "i3", "a2", "a3")
 PIECE = 256
 HEAD = 64
 F32 = jnp.float32
@@ -222,9 +222,11 @@
         if first:
             for cp in smalls[1:-1]:
                 cp.wait()
+        if first:
+            first_wait[1].wait()
+        x_product(layer, size, 0)
+        x_product(layer, size, 1)
         if not first:
-            x_product(layer, size, 0)
-            x_product(layer, size, 1)
             hook()
             x_product(layer, size, 2)
             x_product(layer, size, 3)
@@ -289,15 +291,12 @@
                 state[:, at] = jnp.exp(a_last) * old + exact_dot(bt_stack[r], [part.astype(BF16) for part in split3(tail_x)])
 
         if first:
-            first_wait[1].wait()
-            x_product(layer, size, 0)
-            x_product(layer, size, 1)
             conv(0)
             conv(1)
             first_wait[2].wait()
         plan = ORDER_FIRST if first else ORDER_LATER
         stages = {"x": lambda n: x_product(layer, size, n), "c": conv, "i": inside, "a": across, "z": lambda n: z_product(layer, size, n)}
-        for step in plan.split():
+        for step in plan:
             if step == "wait":
                 first_wait[3].wait()
             else:

time: 58.8 us -> 58.8 us (level)
  no operation moved by 1% of the time
where the time goes in v6:
time: 58.8 us; the launch traced here: 58.6 us
  Pallas kernels  57.6 us (98%)
  local copies, waits for them, and re-layouts  0.97 us (2%)
    pallas_call x1, Pallas kernels, device_forward(): pl.pallas_call(functools.partial(kernel, float(local * tp_size)), out_sha...  57.6 us

profile of v6, /device:TPU:0, one launch (start us, length us, event | category | flops | bytes accessed | tf_op | source)
XLA Modules:
  0.0 58.6 jit_solution(12954642171082477336)
XLA Ops:
  0.0 57.6 %shard_map.145 = bf16[1,256,2048]{2,1,0:T(8,128)(2,1)S(1)} custom-call(bf16[1,256,2048]{2,1,0:T(8,128)(2,1)} %hid_h.1, bf16[2,2048]{1,0:T(2,128)(2,1)} %nw_h.1, bf16[2,2048,1024]{2,1,0:T(8,128)(2,1)} %wz_h.1, bf16[2,2048,1024]{2,1,0:T(8,128)(2,1)} %wx_h.1, bf16[2,2048,128]{2,1,0:T(8,128)(2,1)} %wbc_h.1, bf16[2,16,2048]{2,1,0:T(8,128)(2,1)} %bitcast.1, ...), custom_call_target="tpu_custom_call" | custom-call | tf_op jit(solution)/shard_map/pallas_call | solution.py:491
  57.7 1.0 %copy.17 = bf16[1,256,2048]{2,1,0:T(8,128)(2,1)} copy(bf16[1,256,2048]{2,1,0:T(8,128)(2,1)S(1)} %shard_map.145) | data formatting | bytes 2097152

commit v7 on v6

--- a/solution.py
+++ b/solution.py
@@ -317,16 +317,19 @@
             pstat[core, s + r] = to_row(gate_sq[r * SUB : (r + 1) * SUB])[:, :128]
         if first:
             first_wait[4].wait()
-        for m in range(n_piece):
-            part = dot(gbuf[:size], wo[layer, 1 - core, m])
+        groups = [range(n_piece // 2), range(n_piece // 2, n_piece)] if first else [range(n_piece)]
+        for pieces in groups:
+            for m in pieces:
+                part = dot(gbuf[:size], wo[layer, 1 - core, m])
+                for r in range(subs):
+                    psend[s + r, m] = part[r * SUB : (r + 1) * SUB]
+            if first and pieces[0] == 0:
+                pl.semaphore_wait(barrier, 2)
             for r in range(subs):
-                psend[s + r, m] = part[r * SUB : (r + 1) * SUB]
-        if first:
-            pl.semaphore_wait(barrier, 2)
-        for r in range(subs):
-            pstat_copy(s + r).start()
-            for m in range(n_piece):
-                p_copy(s + r, m).start()
+                if pieces[0] == 0:
+                    pstat_copy(s + r).start()
+                for m in pieces:
+                    p_copy(s + r, m).start()
         if first:
             first_wait[5].wait()
         for m in range(n_piece):

time: 58.8 us -> 58.6 us (level)
  no operation moved by 1% of the time
where the time goes in v7:
time: 58.6 us; the launch traced here: 58.4 us
  Pallas kernels  57.5 us (98%)
  local copies, waits for them, and re-layouts  0.97 us (2%)
    pallas_call x1, Pallas kernels, device_forward(): pl.pallas_call(functools.partial(kernel, float(local * tp_size)), out_sha...  57.5 us

profile of v7, /device:TPU:0, one launch (start us, length us, event | category | flops | bytes accessed | tf_op | source)
XLA Modules:
  0.0 58.4 jit_solution(6195592338211903548)
XLA Ops:
  0.0 57.5 %shard_map.145 = bf16[1,256,2048]{2,1,0:T(8,128)(2,1)S(1)} custom-call(bf16[1,256,2048]{2,1,0:T(8,128)(2,1)} %hid_h.1, bf16[2,2048]{1,0:T(2,128)(2,1)} %nw_h.1, bf16[2,2048,1024]{2,1,0:T(8,128)(2,1)} %wz_h.1, bf16[2,2048,1024]{2,1,0:T(8,128)(2,1)} %wx_h.1, bf16[2,2048,128]{2,1,0:T(8,128)(2,1)} %wbc_h.1, bf16[2,16,2048]{2,1,0:T(8,128)(2,1)} %bitcast.1, ...), custom_call_target="tpu_custom_call" | custom-call | tf_op jit(solution)/shard_map/pallas_call | solution.py:494
  57.5 1.0 %copy.17 = bf16[1,256,2048]{2,1,0:T(8,128)(2,1)} copy(bf16[1,256,2048]{2,1,0:T(8,128)(2,1)S(1)} %shard_map.145) | data formatting | bytes 2097152

commit v8 on v7

--- a/solution.py
+++ b/solution.py
@@ -116,7 +116,7 @@
         return s + m * (s // last)
 
     def p_copy(s, m):
-        return remote(psend.at[s, m], prcv.at[s, m], 0, pr_sem.at[s % 2, m], peer)
+        return remote(psend.at[s, m], prcv.at[s, m], 0, pr_sem.at[s % 2, m // 2], peer)
 
     def pstat_copy(s):
         return remote(pstat.at[core, s], pstat.at[core, s], 1, ptr_sem.at[s % 2], peer)
@@ -348,7 +348,9 @@
         qstat[chip, s] = to_row(chip_sq)[:, :128]
         qstat_copy(s).start()
         for m in range(n_piece):
-            p_copy(s, m).wait_recv()
+            if m % 2 == 0:
+                pair = pl.ds(m, 2)
+                remote(psend.at[s, pair], prcv.at[s, pair], 0, pr_sem.at[s % 2, m // 2], peer).wait_recv()
             qbuf[chip, s, m] = own[m] * f_own + prcv[s, m] * f_peer
             q_copy(s, m).start()
 
@@ -488,7 +490,7 @@
             vm((n_piece, SUB, PIECE), F32), vm((MAX_ROWS, width), BF16), vm((MAX_ROWS + 8, local), F32), vm((MAX_ROWS + 8, bc_width), F32),
             vm((MAX_ROWS, local), F32), vm((MAX_ROWS, local), F32), vm((MAX_ROWS, local), F32), vm((3 * MAX_ROWS, local), BF16), vm((2 * MAX_ROWS + 8, local), F32), vm((HEAD, local), F32), vm((MAX_ROWS, local), BF16),
             pltpu.SemaphoreType.DMA((10,)), pltpu.SemaphoreType.DMA((n_subs,)), pltpu.SemaphoreType.DMA((6,)), pltpu.SemaphoreType.DMA((5,)),
-            pltpu.SemaphoreType.DMA((2, n_piece)), pltpu.SemaphoreType.DMA((steps - 1 + n_piece,)), pltpu.SemaphoreType.DMA((steps - 1 + n_piece,)),
+            pltpu.SemaphoreType.DMA((2, n_piece // 2)), pltpu.SemaphoreType.DMA((steps - 1 + n_piece,)), pltpu.SemaphoreType.DMA((steps - 1 + n_piece,)),
             pltpu.SemaphoreType.DMA((2,)), pltpu.SemaphoreType.DMA((steps,)),
         ]
         return pl.pallas_call(

time: 58.6 us -> 58.6 us (level)
  no operation moved by 1% of the time
where the time goes in v8:
time: 58.6 us; the launch traced here: 58.5 us
  Pallas kernels  57.5 us (98%)
  local copies, waits for them, and re-layouts  0.97 us (2%)
    pallas_call x1, Pallas kernels, device_forward(): pl.pallas_call(functools.partial(kernel, float(local * tp_size)), out_sha...  57.5 us

profile of v8, /device:TPU:0, one launch (start us, length us, event | category | flops | bytes accessed | tf_op | source)
XLA Modules:
  0.0 58.5 jit_solution(10020885698455879420)
XLA Ops:
  0.0 57.5 %shard_map.145 = bf16[1,256,2048]{2,1,0:T(8,128)(2,1)S(1)} custom-call(bf16[1,256,2048]{2,1,0:T(8,128)(2,1)} %hid_h.1, bf16[2,2048]{1,0:T(2,128)(2,1)} %nw_h.1, bf16[2,2048,1024]{2,1,0:T(8,128)(2,1)} %wz_h.1, bf16[2,2048,1024]{2,1,0:T(8,128)(2,1)} %wx_h.1, bf16[2,2048,128]{2,1,0:T(8,128)(2,1)} %wbc_h.1, bf16[2,16,2048]{2,1,0:T(8,128)(2,1)} %bitcast.1, ...), custom_call_target="tpu_custom_call" | custom-call | tf_op jit(solution)/shard_map/pallas_call | solution.py:496
  57.5 1.0 %copy.17 = bf16[1,256,2048]{2,1,0:T(8,128)(2,1)} copy(bf16[1,256,2048]{2,1,0:T(8,128)(2,1)S(1)} %shard_map.145) | data formatting | bytes 2097152
